TPU v7x, 256 devices: a whole 4x4x8 slice. The times are simulated.
256 devices in a mesh: lon: 16 (over x_lo, z), lat: 8 (over y, core), ens: 2 (over x_hi).
Axes of the slice: x: 4 (x_hi: 2, x_lo: 2; x = x_hi * 2 + x_lo), y: 4, z: 8, core: 2. Of those that a mesh axis runs over, the one named last changes fastest.
Arguments:
- inputs: bfloat16 [2, 4, 48, 384, 192], P('ens', None, 'lat', 'lon'), may hold values from -6 to 6
- cotangent: bfloat16 [2, 4, 48, 384, 192], P('ens', None, 'lat', 'lon'), may hold values from -6 to 6
- norm1_gain: float32 [192], replicated, may hold values from 0.25 to 1.75
- norm1_offset: float32 [192], replicated, may hold values from -1.5 to 1.5
- qkv_weight: float32 [192, 576], replicated, may hold values from -0.4375 to 0.4375
- qkv_bias: float32 [576], replicated, may hold values from -1.5 to 1.5
- bias_table: float32 [2, 8, 6, 12, 12, 23], P(None, 'lat'), may hold values from -4 to 302
- proj_weight: float32 [192, 192], replicated, may hold values from -0.4375 to 0.4375
- proj_bias: float32 [192], replicated, may hold values from -1.5 to 1.5
- norm2_gain: float32 [192], replicated, may hold values from 0.25 to 1.75
- norm2_offset: float32 [192], replicated, may hold values from -1.5 to 1.5
- fc1_weight: float32 [192, 768], replicated, may hold values from -0.4375 to 0.4375
- fc1_bias: float32 [768], replicated, may hold values from -1.5 to 1.5
- fc2_weight: float32 [768, 192], replicated, may hold values from -0.21875 to 0.21875
- fc2_bias: float32 [192], replicated, may hold values from -1.5 to 1.5
Outputs:
- block_out: bfloat16 [2, 4, 48, 384, 192], P('ens', None, 'lat', 'lon')
- input_grad: bfloat16 [2, 4, 48, 384, 192], P('ens', None, 'lat', 'lon')
- qkv_weight_grad: float32 [192, 576], P(None, 'lon')
- qkv_bias_grad: float32 [576], P('lon')
- proj_weight_grad: float32 [192, 192], P(None, 'lon')
- proj_bias_grad: float32 [192], P('lon')
- fc1_weight_grad: float32 [192, 768], P(None, 'lon')
- fc1_bias_grad: float32 [768], P('lon')
- fc2_weight_grad: float32 [768, 192], P(None, 'lon')
- fc2_bias_grad: float32 [192], P('lon')
- norm1_gain_grad: float32 [192], P('lon')
- norm1_offset_grad: float32 [192], P('lon')
- norm2_gain_grad: float32 [192], P('lon')
- norm2_offset_grad: float32 [192], P('lon')
- bias_table_grad: float32 [2, 8, 6, 12, 12, 23], P(None, 'lat')
All inputs are finite; a program needn't handle non-finite values.
Results may differ from a plain program's by a relative error of at most 0.025.
Values may be sent and summed in bfloat16 or wider, within the bound.
No kernel may reach another device: no remote copies, remote signals or barrier semaphores. Data moves between devices by JAX's collectives and lax.ppermute only.
A program may use at most 128 MiB of HBM per device.

v0:
```python
import math

import jax
import jax.numpy as jnp
import numpy as np
from jax import lax
from jax.experimental import pallas as pl
from jax.experimental.pallas import tpu as pltpu
from jax.sharding import Mesh
from jax.sharding import PartitionSpec as P

C = 192
HEADS = 6
FF = 768
WO = 12
ROWS = 144
LANES = 896
HX = 72
TAB = 384
EPS = 1e-05
SCALE = 32 ** -0.5
F32 = jnp.float32
BF16 = jnp.bfloat16
FACTOR = 1.0 / math.sqrt(147456)
GELU_A = 0.044715
GELU_C = math.sqrt(2.0 / math.pi)
PART = 128
SLOT = 32


def nn(a, b):
    return lax.dot_general(a, b, (((1,), (0,)), ((), ())), preferred_element_type=F32)


def nt(a, b):
    return lax.dot_general(a, b, (((1,), (1,)), ((), ())), preferred_element_type=F32)


def tn(a, b):
    return lax.dot_general(a, b, (((0,), (0,)), ((), ())), preferred_element_type=F32)


def token_spread():
    out = np.zeros((ROWS, LANES), np.float32)
    for i in range(WO):
        for h in range(HEADS):
            for x in range(WO):
                out[12 * x + i, HX * i + 12 * h + x] = 1.0
    return out


def head_mask():
    out = np.zeros((C, LANES), np.float32)
    for lane in range(12 * HX):
        h = (lane % HX) // 12
        out[32 * h : 32 * h + 32, lane] = 1.0
    return out


def lag_select():
    out = np.zeros((12 * ROWS, TAB), np.float32)
    for i in range(12):
        for y in range(12):
            for j in range(12):
                out[i * ROWS + 12 * y + j, 32 * y + i - j + 11] = 1.0
    return out


def bias_places():
    rows_a = np.zeros((16, 1344), np.float32)
    cols_a = np.zeros((1344, 128), np.float32)
    rows_b = np.zeros((16, 1152), np.float32)
    cols_b = np.zeros((1152, 128), np.float32)
    for n in range(576):
        rows_a[n // 36, n] = 1.0
        cols_a[n, n % 36] = 1.0
    for n in range(768):
        rows_a[n // 48, 576 + n] = 1.0
        cols_a[576 + n, 36 + n % 48] = 1.0
    for k in range(6):
        for n in range(192):
            rows_b[n // 12, 192 * k + n] = 1.0
            cols_b[192 * k + n, 12 * k + n % 12] = 1.0
    return rows_a, cols_a, rows_b, cols_b


def prep_kernel(qkv_ref, proj_ref, fc1_ref, fc2_ref, tab_ref, sel_ref,
                wt_ref, projb_ref, fc1b_ref, fc2b_ref, bias_ref):
    wt_ref[...] = qkv_ref[...].T.astype(BF16)
    projb_ref[...] = proj_ref[...].astype(BF16)
    fc1b_ref[...] = fc1_ref[...].astype(BF16)
    fc2b_ref[...] = fc2_ref[...].astype(BF16)
    tiles = []
    for t in range(3):
        tile = None
        for k in range(4):
            piece = tab_ref[pl.ds(4 * t + k, ROWS, stride=12), :]
            piece = jnp.concatenate([piece, jnp.zeros((ROWS, 105), F32)], axis=1)
            if k:
                piece = pltpu.roll(piece, 32 * k, 1)
            tile = piece if tile is None else tile + piece
        tiles.append(tile)
    table = jnp.concatenate(tiles, axis=1)
    high = table.astype(BF16)
    low = (table - high.astype(F32)).astype(BF16)
    pieces = [[], []]
    for i in range(12):
        sel = sel_ref[ROWS * i : ROWS * i + ROWS, :]
        got = nt(sel, high) + nt(sel, low)
        pieces[0].append(got[:, :HX])
        pieces[1].append(got[:, HX:])
    for v in range(2):
        spare = jnp.zeros((ROWS, LANES - 12 * HX), F32)
        bias_ref[v] = jnp.concatenate(pieces[v] + [spare], axis=1)


def column(row):
    size = row.shape[1]
    eye = lax.broadcasted_iota(jnp.int32, (size, size), 0) == lax.broadcasted_iota(
        jnp.int32, (size, size), 1
    )
    return jnp.sum(jnp.where(eye, row, 0.0), axis=1, keepdims=True)


def window_picks():
    r = lax.broadcasted_iota(jnp.int32, (576, 128), 0).astype(F32)
    m = jnp.floor((r + 0.5) * (1.0 / 12.0))
    j = r - 12.0 * m
    second = m >= 24.0
    n = jnp.where(second, m - 24.0, m)
    src = jnp.where(second, 24.0 * n + 18.0 + j, 24.0 * n + 6.0 + j)
    src = jnp.where(second & (j >= 6.0), 570.0 + 8.0 * n + j, src)
    lane = lax.broadcasted_iota(jnp.int32, (576, 128), 1).astype(F32)
    tiles = [jnp.where(src == lane + 128.0 * t, 1.0, 0.0).astype(BF16) for t in range(6)]
    return jnp.concatenate(tiles, axis=1)


def natural_picks():
    p = lax.broadcasted_iota(jnp.int32, (768, 128), 0).astype(F32)
    own = p < 576.0
    q = p - 576.0
    n = jnp.where(own, jnp.floor((p + 0.5) * (1.0 / 24.0)), jnp.floor((q + 0.5) * 0.125))
    c = jnp.where(own, p - 24.0 * n, q - 8.0 * n)
    inner = jnp.where(c < 18.0, 12.0 * n + c - 6.0, 288.0 + 12.0 * n + c - 18.0)
    inner = jnp.where(c < 6.0, -1.0, inner)
    outer = jnp.where(c < 6.0, 294.0 + 12.0 * n + c, -1.0)
    dst = jnp.where(own, inner, outer)
    lane = lax.broadcasted_iota(jnp.int32, (768, 128), 1).astype(F32)
    tiles = [jnp.where(dst == lane + 128.0 * t, 1.0, 0.0).astype(BF16) for t in range(5)]
    return jnp.concatenate(tiles, axis=1)[:, :576]


def norm_parts(values):
    centre = jnp.sum(values, axis=1, keepdims=True) * (1.0 / C)
    centred = values - centre
    spread = jnp.sum(centred * centred, axis=1, keepdims=True) * (1.0 / C)
    inverse = lax.rsqrt(spread + EPS)
    return centred * inverse, inverse


def norm_back(grad, hat, inverse, gain):
    scaled = grad * gain
    first = jnp.sum(scaled, axis=1, keepdims=True) * (1.0 / C)
    second = jnp.sum(scaled * hat, axis=1, keepdims=True) * (1.0 / C)
    return inverse * (scaled - first - hat * second)


def main_kernel(core_ref, x_ref, cot_ref, n1g_ref, n1o_ref, qb_ref, pb_ref, n2g_ref, n2o_ref,
                f1b_ref, f2b_ref, spread_ref, mask_ref, sel_ref, ra_ref, ca_ref, rb_ref, cb_ref,
                halo_ref, bias_ref, wt_ref, proj_ref, fc1_ref, fc2_ref,
                both_ref, edge_ref, own_ref, send_ref, low_ref, sum_ref, stage_ref, tab_ref):
    n1g, n1o, qb, pb, n2g, n2o, f1b, f2b = (
        ref[...].reshape(1, -1)
        for ref in (n1g_ref, n1o_ref, qb_ref, pb_ref, n2g_ref, n2o_ref, f1b_ref, f2b_ref)
    )
    picks = window_picks()
    xw = nn(picks, jnp.concatenate([x_ref[...], halo_ref[0]], axis=0))
    cw = nn(picks, jnp.concatenate([cot_ref[...], halo_ref[1]], axis=0))
    cot_low = cw.astype(BF16)
    hat1, inv1 = norm_parts(xw)
    normed = (hat1 * n1g + n1o).astype(BF16)
    wq = wt_ref[0:192, :]
    wk = wt_ref[192:384, :]
    wv = wt_ref[384:576, :]
    bq_row = qb[:, 0:192]
    bk_row = qb[:, 192:384]
    bv_row = qb[:, 384:576]
    bq = column(bq_row)
    bk = column(bk_row)
    bv = column(bv_row)
    keys = (nt(normed, wk) + bk_row).astype(BF16)
    values = (nt(normed, wv) + bv_row).astype(BF16)
    spread = spread_ref[...]
    mask = mask_ref[...]
    saved = []
    attended = []
    for g in range(4):
        rows = slice(ROWS * g, ROWS * g + ROWS)
        own = normed[rows]
        query_t = (nt(wq, own) + bq).astype(BF16)
        value_t = (nt(wv, own) + bv).astype(BF16)
        query_bd = nn(query_t, spread).astype(BF16) * mask
        scores = nn(keys[rows], query_bd) * SCALE + bias_ref[g % 2]
        peak = jnp.max(scores, axis=0, keepdims=True)
        raised = jnp.exp(scores - peak)
        total = jnp.sum(raised, axis=0, keepdims=True)
        weights = (raised * (1.0 / total)).astype(BF16)
        mixed = nn(value_t, weights).astype(BF16) * mask
        attended.append(nt(spread, mixed).astype(BF16))
        saved.append((query_bd, weights))
    attended = jnp.concatenate(attended, axis=0)
    attn_out = (nn(attended, proj_ref[...]) + pb).astype(BF16)
    resid = xw + attn_out.astype(F32)
    hat2, inv2 = norm_parts(resid)
    normed2 = (hat2 * n2g + n2o).astype(BF16)
    acts = []
    grads = []
    f1_sums = []
    for g in range(4):
        rows = slice(ROWS * g, ROWS * g + ROWS)
        u = nn(normed2[rows], fc1_ref[...]) + f1b
        square = u * u
        t = jnp.tanh(GELU_C * (u + GELU_A * (square * u)))
        half = 0.5 * (1.0 + t)
        acts.append((u * half).astype(BF16))
        slope = half + 0.5 * u * (1.0 - t * t) * (GELU_C + (3.0 * GELU_A * GELU_C) * square)
        act_grad = nn(cot_low[rows], fc2_ref[...])
        pre = (act_grad * slope).astype(BF16)
        grads.append(pre)
        f1_sums.append(jnp.sum(pre.astype(F32), axis=0, keepdims=True))
    activated = jnp.concatenate(acts, axis=0)
    pre_grad = jnp.concatenate(grads, axis=0)
    f1_sum = f1_sums[0] + f1_sums[1] + f1_sums[2] + f1_sums[3]
    block = (resid + nt(activated, fc2_ref[...]) + f2b).astype(BF16)
    back = natural_picks()
    placed = nn(back, block).astype(BF16)
    both_ref[0] = placed[:576]
    edge_ref[0] = placed[576:]
    n2_grad = nt(pre_grad, fc1_ref[...])
    n2g_sum = jnp.sum(n2_grad * hat2, axis=0, keepdims=True)
    n2o_sum = jnp.sum(n2_grad, axis=0, keepdims=True)
    resid_grad = cw + norm_back(n2_grad, hat2, inv2, n2g)
    attn_grad = resid_grad.astype(BF16)
    pb_sum = jnp.sum(attn_grad.astype(F32), axis=0, keepdims=True)
    f2_sum = jnp.sum(cw, axis=0, keepdims=True)
    grad_q = []
    grad_k = []
    grad_v = []
    for g in range(4):
        rows = slice(ROWS * g, ROWS * g + ROWS)
        query_bd, weights = saved[g]
        own = normed[rows]
        grad_t = nt(proj_ref[...], attn_grad[rows]).astype(BF16)
        grad_bd = nn(grad_t, spread).astype(BF16) * mask
        prob_grad = nn(values[rows], grad_bd)
        probs = weights.astype(F32)
        shared = jnp.sum(probs * prob_grad, axis=0, keepdims=True)
        score_grad = probs * (prob_grad - shared)
        if g < 2:
            sum_ref[g] = score_grad
        else:
            sum_ref[g - 2] += score_grad
        low = score_grad.astype(BF16)
        grad_v.append(nt(weights, grad_bd).astype(BF16))
        grad_k.append((nt(low, query_bd) * SCALE).astype(BF16))
        key_t = (nt(wk, own) + bk).astype(BF16)
        mixed = (nn(key_t, low) * SCALE).astype(BF16) * mask
        grad_q.append(nt(spread, mixed).astype(BF16))
    dq = jnp.concatenate(grad_q, axis=0)
    dk = jnp.concatenate(grad_k, axis=0)
    dv = jnp.concatenate(grad_v, axis=0)
    n1_grad = nn(dq, wq) + nn(dk, wk) + nn(dv, wv)
    n1g_sum = jnp.sum(n1_grad * hat1, axis=0, keepdims=True)
    n1o_sum = jnp.sum(n1_grad, axis=0, keepdims=True)
    input_grad = (resid_grad + norm_back(n1_grad, hat1, inv1, n1g)).astype(BF16)
    placed = nn(back, input_grad).astype(BF16)
    both_ref[1] = placed[:576]
    edge_ref[1] = placed[576:]
    sums = [jnp.sum(d.astype(F32), axis=0, keepdims=True) for d in (dq, dk, dv)]
    for v in range(2):
        turned = sum_ref[v].T
        total = jnp.zeros((HX, TAB), F32)
        for i in range(12):
            piece = turned[HX * i : HX * i + HX, :].astype(BF16)
            total = total + nn(piece, sel_ref[ROWS * i : ROWS * i + ROWS, :])
        for t in range(3):
            tab_ref[ROWS * t + HX * v : ROWS * t + HX * v + HX, :] = total[:, 128 * t : 128 * t + 128]
    tab_ref[3 * ROWS :, :] = jnp.zeros((16 * SLOT - 3 * ROWS, 128), F32)
    low_ref[...] = tab_ref[...].astype(BF16)
    dw_q = tn(dq, normed)
    dw_k = tn(dk, normed)
    dw_v = tn(dv, normed)
    dw_qkv = jnp.concatenate([dw_q, dw_k, dw_v], axis=0)
    dw_p = tn(attn_grad, attended)
    dw_1 = tn(pre_grad, normed2)
    dw_2 = tn(cot_low, activated)
    vec_a = jnp.concatenate(sums + [f1_sum[:, 0:192], f1_sum[:, 192:384], f1_sum[:, 384:576], f1_sum[:, 576:768]], axis=1)
    vec_b = jnp.concatenate([pb_sum, f2_sum, n1g_sum, n1o_sum, n2g_sum, n2o_sum], axis=1)
    row_a = nn((ra_ref[...].astype(F32) * vec_a).astype(BF16), ca_ref[...])
    row_b = nn((rb_ref[...].astype(F32) * vec_b).astype(BF16), cb_ref[...])
    for l in range(16):
        a36 = dw_qkv[36 * l : 36 * l + 36]
        a12 = dw_p[12 * l : 12 * l + 12]
        b48 = dw_1[48 * l : 48 * l + 48]
        d12 = dw_2[12 * l : 12 * l + 12]
        top = PART * l
        stage_ref[0, top : top + 36, :] = a36[:, :128]
        stage_ref[0, top + 36 : top + 48, :] = a12[:, :128]
        a_rest = jnp.concatenate([a36[:, 128:], a12[:, 128:]], axis=0)
        stage_ref[0, top + 48 : top + 96, :] = jnp.concatenate([a_rest, b48[:, 128:]], axis=1)
        stage_ref[0, top + 96 : top + 108, :] = d12[:, 640:]
        stage_ref[0, top + 108 : top + 112, :] = jnp.zeros((4, 128), F32)
        stage_ref[0, top + 112 : top + 128, :] = jnp.concatenate(
            [row_a[l : l + 1], row_b[l : l + 1], jnp.zeros((14, 128), F32)], axis=0
        )
        stage_ref[1, top : top + 48, :] = b48[:, :128]
        for b in range(5):
            piece = d12[:, 128 * b : 128 * b + 128]
            stage_ref[1, top + 48 + 16 * b : top + 64 + 16 * b, :] = jnp.concatenate(
                [piece, jnp.zeros((4, 128), F32)], axis=0
            )
    core = core_ref[0]
    for k in range(8):
        for l in range(16):
            rows = slice(PART * l + 16 * k, PART * l + 16 * k + 16)
            spot = slice(16 * l, 16 * l + 16)
            own_ref[k, spot, :] = stage_ref[core, rows, :].astype(BF16)
            send_ref[k, spot, :] = stage_ref[1 - core, rows, :].astype(BF16)


def join_kernel(own_ref, got_ref, out_ref):
    out_ref[...] = (own_ref[...].astype(F32) + got_ref[...].astype(F32)).astype(BF16)


def band_sum_kernel(in_ref, tab_ref, twin_ref, out_ref):
    total = in_ref[0].astype(F32)
    for k in range(1, 8):
        total = total + in_ref[k].astype(F32)
    low = total.astype(BF16)
    table = (tab_ref[...].astype(F32) + twin_ref[...].astype(F32)).astype(BF16)
    for l in range(16):
        out_ref[l, 0:16, :] = low[16 * l : 16 * l + 16]
        out_ref[l, 16:, :] = table[SLOT * l : SLOT * l + SLOT]


def lon_sum_kernel(in_ref, part_ref, tab_ref):
    total = in_ref[0].astype(F32)
    for l in range(1, 16):
        total = total + in_ref[l].astype(F32)
    low = total.astype(BF16)
    for k in range(16):
        part_ref[k] = low[:16]
        tab_ref[k] = low[16:]


def final_kernel(part_ref, tab_ref, qw_ref, pw_ref, f1_ref, f2_ref, qb_ref, pb_ref, f1b_ref, f2b_ref,
                 n1g_ref, n1o_ref, n2g_ref, n2o_ref, out_tab_ref):
    def half(core):
        rows = [part_ref[4 * y + 2 * core + e] for y in range(4) for e in range(2)]
        return jnp.concatenate(rows, axis=0).astype(F32) * FACTOR

    first = half(0)
    second = half(1)
    a = jnp.concatenate([first[0:48], first[48:96, 0:64]], axis=1)
    qw_ref[...] = a[0:36]
    pw_ref[...] = a[36:48]
    f1_ref[...] = jnp.concatenate([second[0:48], first[48:96, 64:128]], axis=1)
    d = [second[48 + 16 * k : 60 + 16 * k] for k in range(5)] + [first[96:108]]
    f2_ref[...] = jnp.concatenate(d, axis=1)
    va = first[112:113]
    vb = first[113:114]
    qb_ref[...] = va[:, 0:36].reshape(36)
    f1b_ref[...] = va[:, 36:84].reshape(48)
    for k, ref in enumerate((pb_ref, f2b_ref, n1g_ref, n1o_ref, n2g_ref, n2o_ref)):
        ref[...] = vb[:, 12 * k : 12 * k + 12].reshape(12)
    tab = tab_ref[...].astype(F32)
    for t in range(3):
        tile = tab[ROWS * t : ROWS * t + ROWS]
        for k in range(4):
            piece = pltpu.roll(tile, 128 - 32 * k, 1) if k else tile
            out_tab_ref[pl.ds(4 * t + k, ROWS, stride=12), :] = piece[:, :23]


def call(kernel, out_shape, smem=0, far=0, near=0, limit=8, scratch=()):
    count = smem + far + near
    specs = [pl.BlockSpec(memory_space=pltpu.SMEM)] * smem + [
        pl.BlockSpec(memory_space=pltpu.VMEM)
    ] * (far + near)
    run = pl.pallas_call(
        kernel,
        out_shape=out_shape,
        in_specs=specs,
        out_specs=jax.tree.map(lambda _: pl.BlockSpec(memory_space=pltpu.VMEM), out_shape),
        scratch_shapes=scratch,
        compiler_params=pltpu.CompilerParams(vmem_limit_bytes=limit << 20),
    )

    def go(*args):
        kept = args[: smem + far] + tuple(
            pltpu.with_memory_space_constraint(a, pltpu.VMEM) for a in args[smem + far :]
        )
        assert len(args) == count
        return run(*kept)

    return go


def near(dims, dtype):
    return pltpu.VMEM(dims, dtype)


def shape(dims, dtype):
    return jax.ShapeDtypeStruct(dims, dtype)


def on_device(inputs, cotangent, norm1_gain, norm1_offset, qkv_weight, qkv_bias, bias_table,
              proj_weight, proj_bias, norm2_gain, norm2_offset, fc1_weight, fc1_bias,
              fc2_weight, fc2_bias):
    grid = inputs.shape
    x = inputs.reshape(576, C)
    cot = cotangent.reshape(576, C)
    edge = jnp.stack([inputs[0, :, :, :8, :].reshape(192, C), cotangent[0, :, :, :8, :].reshape(192, C)])
    halo = lax.ppermute(edge, "lon", [(k, (k - 1) % 16) for k in range(16)])
    spread = jnp.asarray(token_spread(), BF16)
    mask = jnp.asarray(head_mask(), BF16)
    sel = jnp.asarray(lag_select(), BF16)
    ra, ca, rb, cb = (jnp.asarray(a, BF16) for a in bias_places())
    table = bias_table.reshape(12 * ROWS, 23)
    wt, proj, fc1, fc2, bias = call(
        prep_kernel,
        [near((576, C), BF16), near((C, C), BF16), near((C, FF), BF16), near((C, FF), BF16),
         near((2, ROWS, LANES), F32)],
        far=6,
        limit=16,
    )(qkv_weight, proj_weight, fc1_weight, fc2_weight.T, table, sel)
    core = lax.axis_index("core").astype(jnp.int32).reshape(1)
    both, ends, own, send, tab = call(
        main_kernel,
        [shape((2, 576, C), BF16), near((2, 192, C), BF16), near((8, 256, 128), BF16),
         near((8, 256, 128), BF16), near((16 * SLOT, 128), BF16)],
        smem=1,
        far=17,
        near=6,
        limit=36,
        scratch=[pltpu.VMEM((2, ROWS, LANES), F32), pltpu.VMEM((2, 16 * PART, 128), F32),
                 pltpu.VMEM((16 * SLOT, 128), F32)],
    )(core, x, cot, norm1_gain, norm1_offset, qkv_bias, proj_bias,
      norm2_gain, norm2_offset, fc1_bias, fc2_bias, spread, mask, sel, ra, ca, rb, cb,
      halo, bias, wt, proj, fc1, fc2)
    got = lax.ppermute(send, "core", [(0, 1), (1, 0)])
    twin = lax.ppermute(tab, "ens", [(0, 1), (1, 0)])
    home = lax.ppermute(ends, "lon", [(k, (k + 1) % 16) for k in range(16)])
    joined = call(join_kernel, near((8, 256, 128), BF16), near=2)(own, got)
    bands = lax.all_to_all(joined, ("y", "ens"), split_axis=0, concat_axis=0, tiled=True)
    merged = call(band_sum_kernel, near((16, 16 + SLOT, 128), BF16), near=3)(bands, tab, twin)
    arrived = lax.all_to_all(merged, "lon", split_axis=0, concat_axis=0, tiled=True)
    part, tab_copies = call(
        lon_sum_kernel, [near((16, 16, 128), BF16), near((16, SLOT, 128), BF16)], near=1
    )(arrived)
    parts = lax.all_to_all(part, ("y", "core", "ens"), split_axis=0, concat_axis=0, tiled=True)
    tab_all = lax.all_to_all(tab_copies, "lon", split_axis=0, concat_axis=0, tiled=True)
    qw, pw, f1, f2, qb, pb, f1b, f2b, n1g, n1o, n2g, n2o, tab_out = call(
        final_kernel,
        [shape((36, C), F32), shape((12, C), F32), shape((48, C), F32), shape((12, FF), F32),
         shape((36,), F32), shape((12,), F32), shape((48,), F32)] + [shape((12,), F32)] * 5
        + [shape((12 * ROWS, 23), F32)],
        near=2,
    )(parts, tab_all.reshape(16 * SLOT, 128))
    full = both.reshape(2, *grid[1:])
    ends = home.reshape(2, grid[1], grid[2], 8, C)[:, :, :, :6]
    full = jnp.concatenate([ends, full[:, :, :, 6:]], axis=3)
    return (full[0][None], full[1][None], qw.T, qb, pw.T, pb, f1.T, f1b, f2.T, f2b, n1g, n1o, n2g, n2o,
            tab_out.reshape(bias_table.shape))


def solution(mesh):
    split = Mesh(mesh.devices.reshape(16, 4, 2, 2), ("lon", "y", "core", "ens"))
    lat = ("y", "core")
    tokens = P("ens", None, lat, "lon", None)
    table = P(None, lat, None, None, None, None)
    return jax.shard_map(
        on_device,
        mesh=split,
        in_specs=(tokens, tokens, P(), P(), P(), P(), table) + (P(),) * 8,
        out_specs=(tokens, tokens, P(None, "lon"), P("lon"), P(None, "lon"), P("lon"), P(None, "lon"),
                   P("lon"), P(None, "lon"), P("lon"), P("lon"), P("lon"), P("lon"), P("lon"), table),
        check_vma=False,
    )
```

profile of v0, /device:TPU:1, one launch (start us, length us, event | category | flops | bytes accessed | tf_op | source)
XLA Modules:
  0.0 91.4 jit_solution(11922611009849484054)
XLA Ops:
  0.6 0.9 slice.18
  1.5 0.9 slice.19
  2.5 7.4 %collective-permute-start = (bf16[2,192,192]{2,1,0:T(8,128)(2,1)S(1)}, bf16[2,192,192]{2,1,0:T(8,128)(2,1)S(1)}, u32[]{:S(2)}, u32[]{:S(2)}) collective-permute-start(bf16[2,192,192]{2,1,0:T(8,128)(2,1)S(1)} %pad_maximum_fusion.1), channel_id=1, source_target_pairs={{0,240},{16,0},{32,16},{48,32},{64,48},{80,64},{96,80},{112,96},{1... | collective-permute-start | bytes 442376 | tf_op jit(solution)/shard_map/ppermute | solution.py:423
  9.9 0.0 copy-start
  9.9 1.3 %copy-done = bf16[1728,384]{1,0:T(8,128)(2,1)S(1)} copy-done((bf16[1728,384]{1,0:T(8,128)(2,1)S(1)}, bf16[1728,384]{1,0:T(8,128)(2,1)}, u32[]{:S(2)}) %copy-start) | copy-done | bytes 1327128
  11.2 0.0 copy-start.2
  11.2 1.2 %copy-done.2 = f32[2,1,6,12,12,23]{5,1,4,3,2,0:T(1,128)S(1)} copy-done((f32[2,1,6,12,12,23]{5,1,4,3,2,0:T(1,128)S(1)}, f32[2,1,6,12,12,23]{5,1,4,3,2,0:T(1,128)}, u32[]{:S(2)}) %copy-start.2) | copy-done | bytes 159000
  12.4 0.0 copy-start.3
  12.4 1.1 %copy-done.3 = f32[192,768]{1,0:T(8,128)S(1)} copy-done((f32[192,768]{1,0:T(8,128)S(1)}, f32[192,768]{1,0:T(8,128)}, u32[]{:S(2)}) %copy-start.3) | copy-done | bytes 589848
  13.4 1.1 %copy-done.4 = f32[768,192]{0,1:T(8,128)S(1)} copy-done((f32[768,192]{0,1:T(8,128)S(1)}, f32[768,192]{0,1:T(8,128)}, u32[]{:S(2)}) %copy-start.4) | copy-done | bytes 589848
  14.5 1.0 %copy-done.7 = f32[192,576]{1,0:T(8,128)S(1)} copy-done((f32[192,576]{1,0:T(8,128)S(1)}, f32[192,576]{1,0:T(8,128)}, u32[]{:S(2)}) %copy-start.7) | copy-done | bytes 442392
  15.5 0.9 %copy-done.12 = f32[192,192]{1,0:T(8,128)S(1)} copy-done((f32[192,192]{1,0:T(8,128)S(1)}, f32[192,192]{1,0:T(8,128)}, u32[]{:S(2)}) %copy-start.12) | copy-done | bytes 147480
  16.5 0.0 copy-start.9
  16.5 0.0 copy-start.10
  16.5 0.0 copy-start.11
  16.5 0.0 copy-start.13
  16.5 0.0 copy-start.14
  16.5 0.0 copy-start.15
  16.5 0.0 copy-start.16
  16.6 0.0 copy-start.17
  16.6 0.0 copy-start.18
  16.6 0.0 copy-start.19
  16.6 0.0 copy-start.20
  16.6 0.0 copy-start.21
  16.6 0.0 copy-start.22
  16.6 1.4 %shard_map.325 = (bf16[576,192]{1,0:T(8,128)(2,1)S(1)}, bf16[192,192]{1,0:T(8,128)(2,1)S(1)}, bf16[192,768]{1,0:T(8,128)(2,1)S(1)}, bf16[192,768]{1,0:T(8,128)(2,1)S(1)}, f32[2,144,896]{2,1,0:T(8,128)S(1)}) custom-call(f32[192,576]{1,0:T(8,128)S(1)} %copy-done.7, f32[192,192]{1,0:T(8,128)S(1)} %copy-done.12, f32[192,768]{1,0:T(8,128)S(1)} %copy-done.3, ...), custom_call_target="tpu_custom_call" | custom-call | tf_op jit(solution)/shard_map/pallas_call | solution.py:403
  18.1 0.0 collective-permute-done.halo_ref
  18.1 0.0 copy-done.1
  18.1 0.0 copy-done.5
  18.1 0.0 copy-done.6
  18.1 0.0 copy-done.8
  18.1 0.0 copy-done.9
  18.1 0.1 copy-done.10
  18.2 0.1 copy-done.11
  18.3 0.0 copy-done.13
  18.3 0.0 copy-done.14
  18.3 0.0 copy-done.15
  18.3 0.0 copy-done.16
  18.3 0.0 copy-done.17
  18.3 0.0 copy-done.18
  18.3 0.0 copy-done.19
  18.3 0.0 copy-done.20
  18.3 0.0 copy-done.21
  18.3 0.0 copy-done.22
  18.4 13.7 %shard_map.326 = (bf16[2,576,192]{2,1,0:T(8,128)(2,1)S(1)}, bf16[2,192,192]{2,1,0:T(8,128)(2,1)S(1)}, bf16[8,256,128]{2,1,0:T(8,128)(2,1)S(1)}, bf16[8,256,128]{2,1,0:T(8,128)(2,1)S(1)}, bf16[512,128]{1,0:T(8,128)(2,1)S(1)}) custom-call(s32[1]{0:T(128)} %bitcast.core_ref, bf16[576,192]{1,0:T(8,128)(2,1)S(1)} %bitcast.20, bf16[576,192]{1,0:T(8,128)(2,1)S(1)} %bitcast.21, ...), custom_call_target="tpu_custom_call" | custom-call | tf_op jit(solution)/shard_map/pallas_call | solution.py:403
  32.1 1.0 %collective-permute-start.2 = (bf16[8,256,128]{2,1,0:T(8,128)(2,1)S(1)}, bf16[8,256,128]{2,1,0:T(8,128)(2,1)S(1)}, u32[]{:S(2)}, u32[]{:S(2)}) collective-permute-start(bf16[8,256,128]{2,1,0:T(8,128)(2,1)S(1)} %get-tuple-element.48), channel_id=1, source_target_pairs={{0,2},{2,0},{1,3},{3,1},{4,6},{6,4},{5,7},{7,5},{8,10},{10,8},{9,1... | collective-permute-start | bytes 1572872 | tf_op jit(solution)/shard_map/ppermute | solution.py:450
  33.1 1.5 %collective-permute-done.2.got_ref = bf16[8,256,128]{2,1,0:T(8,128)(2,1)S(1)} collective-permute-done((bf16[8,256,128]{2,1,0:T(8,128)(2,1)S(1)}, bf16[8,256,128]{2,1,0:T(8,128)(2,1)S(1)}, u32[]{:S(2)}, u32[]{:S(2)}) %collective-permute-start.2) | collective-permute-done | bytes 524320 | tf_op jit(solution)/shard_map/ppermute | solution.py:450
  34.6 0.9 shard_map.327
  35.6 6.4 %all-to-all-start = ((bf16[8,256,128]{2,1,0:T(8,128)(2,1)}), bf16[8,256,128]{2,1,0:T(8,128)(2,1)S(1)}, u32[]{:S(2)}, u32[]{:S(2)}) async-start(bf16[8,256,128]{2,1,0:T(8,128)(2,1)} %shard_map.327), calls=%async_computation | async-start | bytes 1048576 | tf_op jit(solution)/shard_map/all_to_all | solution.py:454
  41.9 3.0 %collective-permute-start.3 = (bf16[512,128]{1,0:T(8,128)(2,1)S(1)}, bf16[512,128]{1,0:T(8,128)(2,1)S(1)}, u32[]{:S(2)}, u32[]{:S(2)}) collective-permute-start(bf16[512,128]{1,0:T(8,128)(2,1)S(1)} %get-tuple-element.49.tab_ref), channel_id=1, source_target_pairs={{0,1},{1,0},{2,3},{3,2},{4,5},{5,4},{6,7},{7,6},{8,9},{9,8},{10,11... | collective-permute-start | bytes 393224 | tf_op jit(solution)/shard_map/ppermute | solution.py:451
  44.9 8.8 %collective-permute-done.3.twin_ref = bf16[512,128]{1,0:T(8,128)(2,1)S(1)} collective-permute-done((bf16[512,128]{1,0:T(8,128)(2,1)S(1)}, bf16[512,128]{1,0:T(8,128)(2,1)S(1)}, u32[]{:S(2)}, u32[]{:S(2)}) %collective-permute-start.3) | collective-permute-done | bytes 131104 | tf_op jit(solution)/shard_map/ppermute | solution.py:451
  53.6 0.0 all-to-all-done.in_ref
  53.6 0.1 shard_map.328
  53.7 10.1 %all_to_all.20.in_ref = bf16[16,48,128]{2,1,0:T(8,128)(2,1)S(1)} all-to-all(bf16[16,48,128]{2,1,0:T(8,128)(2,1)S(1)} %shard_map.328), channel_id=1, replica_groups=mesh['lon'=16,'y'=4,'core'=2,'ens'=2] {'lon'}, dimensions={0} | all-to-all | bytes 393216 | tf_op jit(solution)/shard_map/all_to_all | solution.py:456
  63.8 0.7 shard_map.329
  64.5 7.4 %all-to-all-start.2 = ((bf16[16,16,128]{2,1,0:T(8,128)(2,1)}), bf16[16,16,128]{2,1,0:T(8,128)(2,1)S(1)}, u32[]{:S(2)}, u32[]{:S(2)}) async-start(bf16[16,16,128]{2,1,0:T(8,128)(2,1)} %get-tuple-element.50), calls=%async_computation.2 | async-start | bytes 131072 | tf_op jit(solution)/shard_map/all_to_all | solution.py:460
  71.9 1.4 %collective-permute-start.1 = (bf16[2,192,192]{2,1,0:T(8,128)(2,1)S(1)}, bf16[2,192,192]{2,1,0:T(8,128)(2,1)S(1)}, u32[]{:S(2)}, u32[]{:S(2)}) collective-permute-start(bf16[2,192,192]{2,1,0:T(8,128)(2,1)S(1)} %get-tuple-element.45), channel_id=1, source_target_pairs={{0,16},{16,32},{32,48},{48,64},{64,80},{80,96},{96,112},{112,128},... | collective-permute-start | bytes 442376 | tf_op jit(solution)/shard_map/ppermute | solution.py:452
  73.4 6.0 %all-to-all-done.2.part_ref = bf16[16,16,128]{2,1,0:T(8,128)(2,1)S(1)} async-done(((bf16[16,16,128]{2,1,0:T(8,128)(2,1)}), bf16[16,16,128]{2,1,0:T(8,128)(2,1)S(1)}, u32[]{:S(2)}, u32[]{:S(2)}) %all-to-all-start.2) | async-done | bytes 65568 | tf_op jit(solution)/shard_map/all_to_all | solution.py:460
  79.4 3.5 %all-to-all-start.3 = ((bf16[16,32,128]{2,1,0:T(8,128)(2,1)}), bf16[16,32,128]{2,1,0:T(8,128)(2,1)S(1)}, u32[]{:S(2)}, u32[]{:S(2)}) async-start(bf16[16,32,128]{2,1,0:T(8,128)(2,1)} %get-tuple-element.51), calls=%async_computation.3 | async-start | bytes 262144 | tf_op jit(solution)/shard_map/all_to_all | solution.py:461
  82.9 0.3 slice.25
  83.2 0.0 collective-permute-done.1
  83.2 1.1 %pad_maximum_fusion = (bf16[1,4,6,24,192]{4,3,2,1,0:T(8,128)(2,1)}, bf16[1,4,6,24,192]{4,3,2,1,0:T(8,128)(2,1)}) fusion(bf16[2,4,6,18,192]{4,3,2,1,0:T(8,128)(2,1)S(1)} %slice.25, bf16[2,4,6,6,192]{4,3,2,1,0:T(8,128)(2,1)S(1)} %bitcast.24), kind=kLoop, calls=%fused_computation.3 | loop fusion | flops 884736 | bytes 884736 | tf_op jit(solution)/shard_map/concatenate | solution.py:471
  84.3 6.0 %all-to-all-done.3 = bf16[16,32,128]{2,1,0:T(8,128)(2,1)S(1)} async-done(((bf16[16,32,128]{2,1,0:T(8,128)(2,1)}), bf16[16,32,128]{2,1,0:T(8,128)(2,1)S(1)}, u32[]{:S(2)}, u32[]{:S(2)}) %all-to-all-start.3) | async-done | bytes 131104 | tf_op jit(solution)/shard_map/all_to_all | solution.py:461
  90.3 1.1 %shard_map.330 = (f32[36,192]{1,0:T(8,128)}, f32[12,192]{1,0:T(8,128)}, f32[48,192]{1,0:T(8,128)}, f32[12,768]{1,0:T(8,128)}, f32[36]{0:T(128)}, /*index=5*/f32[...) custom-call(bf16[16,16,128]{2,1,0:T(8,128)(2,1)S(1)} %all-to-all-don, ...), custom_call_target="tpu_custom_call" | custom-call | tf_op jit(solution)/shard_map/pallas_call | solution.py:403
  (8 shorter events, 0.0 us)
Async XLA Ops:
  2.5 15.6 %collective-permute-start = (bf16[2,192,192]{2,1,0:T(8,128)(2,1)S(1)}, bf16[2,192,192]{2,1,0:T(8,128)(2,1)S(1)}, u32[]{:S(2)}, u32[]{:S(2)}) collective-permute-start(bf16[2,192,192]{2,1,0:T(8,128)(2,1)S(1)} %pad_maximum_fusion.1), channel_id=1, source_target_pairs={{0,240},{16,0},{32,16},{48,32},{64,48},{80,64},{96,80},{112,96},{1... | collective-permute-start | bytes 442376 | tf_op jit(solution)/shard_map/ppermute | solution.py:423
  9.9 1.3 %copy-start = (bf16[1728,384]{1,0:T(8,128)(2,1)S(1)}, bf16[1728,384]{1,0:T(8,128)(2,1)}, u32[]{:S(2)}) copy-start(bf16[1728,384]{1,0:T(8,128)(2,1)} %constant.20.clone.sel_ref) | copy-start | bytes 3981316
  11.2 1.2 %copy-start.2 = (f32[2,1,6,12,12,23]{5,1,4,3,2,0:T(1,128)S(1)}, f32[2,1,6,12,12,23]{5,1,4,3,2,0:T(1,128)}, u32[]{:S(2)}) copy-start(f32[2,1,6,12,12,23]{5,1,4,3,2,0:T(1,128)} %param.28) | copy-start | bytes 476932
  12.4 1.1 %copy-start.3 = (f32[192,768]{1,0:T(8,128)S(1)}, f32[192,768]{1,0:T(8,128)}, u32[]{:S(2)}) copy-start(f32[192,768]{1,0:T(8,128)} %fc1_ref.1) | copy-start | bytes 1769476
  13.4 1.1 %copy-start.4 = (f32[768,192]{0,1:T(8,128)S(1)}, f32[768,192]{0,1:T(8,128)}, u32[]{:S(2)}) copy-start(f32[768,192]{0,1:T(8,128)} %param.35) | copy-start | bytes 1769476
  14.5 1.0 %copy-start.7 = (f32[192,576]{1,0:T(8,128)S(1)}, f32[192,576]{1,0:T(8,128)}, u32[]{:S(2)}) copy-start(f32[192,576]{1,0:T(8,128)} %qkv_ref.1) | copy-start | bytes 1327108
  15.5 0.9 %copy-start.12 = (f32[192,192]{1,0:T(8,128)S(1)}, f32[192,192]{1,0:T(8,128)}, u32[]{:S(2)}) copy-start(f32[192,192]{1,0:T(8,128)} %proj_ref.1) | copy-start | bytes 442372
  16.5 1.6 %copy-start.1 = (bf16[1728,384]{1,0:T(8,128)(2,1)S(1)}, bf16[1728,384]{1,0:T(8,128)(2,1)}, u32[]{:S(2)}) copy-start(bf16[1728,384]{1,0:T(8,128)(2,1)} %constant.20.clone.sel_ref) | copy-start | bytes 3981316
  16.5 1.6 %copy-start.5 = (bf16[1,4,6,24,192]{4,3,2,1,0:T(8,128)(2,1)S(1)}, bf16[1,4,6,24,192]{4,3,2,1,0:T(8,128)(2,1)}, u32[]{:S(2)}) copy-start(bf16[1,4,6,24,192]{4,3,2,1,0:T(8,128)(2,1)} %param.22) | copy-start | bytes 663556
  16.5 1.6 %copy-start.6 = (bf16[1,4,6,24,192]{4,3,2,1,0:T(8,128)(2,1)S(1)}, bf16[1,4,6,24,192]{4,3,2,1,0:T(8,128)(2,1)}, u32[]{:S(2)}) copy-start(bf16[1,4,6,24,192]{4,3,2,1,0:T(8,128)(2,1)} %param.23) | copy-start | bytes 663556
  16.5 1.6 %copy-start.8 = (bf16[1344,128]{1,0:T(8,128)(2,1)S(1)}, bf16[1344,128]{1,0:T(8,128)(2,1)}, u32[]{:S(2)}) copy-start(bf16[1344,128]{1,0:T(8,128)(2,1)} %constant.22.clone.ca_ref) | copy-start | bytes 1032196
  16.5 1.6 %copy-start.9 = (bf16[192,896]{1,0:T(8,128)(2,1)S(1)}, bf16[192,896]{1,0:T(8,128)(2,1)}, u32[]{:S(2)}) copy-start(bf16[192,896]{1,0:T(8,128)(2,1)} %constant.19.clone.mask_ref) | copy-start | bytes 1032196
  16.5 1.7 %copy-start.10 = (bf16[1152,128]{1,0:T(8,128)(2,1)S(1)}, bf16[1152,128]{1,0:T(8,128)(2,1)}, u32[]{:S(2)}) copy-start(bf16[1152,128]{1,0:T(8,128)(2,1)} %constant.24.clone.cb_ref) | copy-start | bytes 884740
  16.5 1.8 %copy-start.11 = (bf16[144,896]{1,0:T(8,128)(2,1)S(1)}, bf16[144,896]{1,0:T(8,128)(2,1)}, u32[]{:S(2)}) copy-start(bf16[144,896]{1,0:T(8,128)(2,1)} %constant.18.clone.spread_ref) | copy-start | bytes 774148
  16.5 1.8 %copy-start.13 = (bf16[16,1344]{1,0:T(8,128)(2,1)S(1)}, bf16[16,1344]{1,0:T(8,128)(2,1)}, u32[]{:S(2)}) copy-start(bf16[16,1344]{1,0:T(8,128)(2,1)} %constant.21.clone.ra_ref) | copy-start | bytes 129028
  16.5 1.8 %copy-start.14 = (bf16[16,1152]{1,0:T(8,128)(2,1)S(1)}, bf16[16,1152]{1,0:T(8,128)(2,1)}, u32[]{:S(2)}) copy-start(bf16[16,1152]{1,0:T(8,128)(2,1)} %constant.23.clone.rb_ref) | copy-start | bytes 110596
  16.5 1.8 %copy-start.15 = (f32[576]{0:T(1024)S(1)}, f32[576]{0:T(1024)}, u32[]{:S(2)}) copy-start(f32[576]{0:T(1024)} %qb_ref.1) | copy-start | bytes 6916
  16.5 1.7 %copy-start.16 = (f32[768]{0:T(1024)S(1)}, f32[768]{0:T(1024)}, u32[]{:S(2)}) copy-start(f32[768]{0:T(1024)} %f1b_ref.1) | copy-start | bytes 9220
  16.6 1.7 %copy-start.17 = (f32[192]{0:T(256)S(1)}, f32[192]{0:T(256)}, u32[]{:S(2)}) copy-start(f32[192]{0:T(256)} %n1g_ref.1) | copy-start | bytes 2308
  16.6 1.7 %copy-start.18 = (f32[192]{0:T(256)S(1)}, f32[192]{0:T(256)}, u32[]{:S(2)}) copy-start(f32[192]{0:T(256)} %n1o_ref.1) | copy-start | bytes 2308
  16.6 1.7 %copy-start.19 = (f32[192]{0:T(256)S(1)}, f32[192]{0:T(256)}, u32[]{:S(2)}) copy-start(f32[192]{0:T(256)} %pb_ref.1) | copy-start | bytes 2308
  16.6 1.7 %copy-start.20 = (f32[192]{0:T(256)S(1)}, f32[192]{0:T(256)}, u32[]{:S(2)}) copy-start(f32[192]{0:T(256)} %n2g_ref.1) | copy-start | bytes 2308
  16.6 1.7 %copy-start.21 = (f32[192]{0:T(256)S(1)}, f32[192]{0:T(256)}, u32[]{:S(2)}) copy-start(f32[192]{0:T(256)} %n2o_ref.1) | copy-start | bytes 2308
  16.6 1.7 %copy-start.22 = (f32[192]{0:T(256)S(1)}, f32[192]{0:T(256)}, u32[]{:S(2)}) copy-start(f32[192]{0:T(256)} %f2b_ref.1) | copy-start | bytes 2308
  32.1 2.6 %collective-permute-start.2 = (bf16[8,256,128]{2,1,0:T(8,128)(2,1)S(1)}, bf16[8,256,128]{2,1,0:T(8,128)(2,1)S(1)}, u32[]{:S(2)}, u32[]{:S(2)}) collective-permute-start(bf16[8,256,128]{2,1,0:T(8,128)(2,1)S(1)} %get-tuple-element.48), channel_id=1, source_target_pairs={{0,2},{2,0},{1,3},{3,1},{4,6},{6,4},{5,7},{7,5},{8,10},{10,8},{9,1... | collective-permute-start | bytes 1572872 | tf_op jit(solution)/shard_map/ppermute | solution.py:450
  35.6 18.1 %all-to-all-start = ((bf16[8,256,128]{2,1,0:T(8,128)(2,1)}), bf16[8,256,128]{2,1,0:T(8,128)(2,1)S(1)}, u32[]{:S(2)}, u32[]{:S(2)}) async-start(bf16[8,256,128]{2,1,0:T(8,128)(2,1)} %shard_map.327), calls=%async_computation | async-start | bytes 1048576 | tf_op jit(solution)/shard_map/all_to_all | solution.py:454
  41.9 11.7 %collective-permute-start.3 = (bf16[512,128]{1,0:T(8,128)(2,1)S(1)}, bf16[512,128]{1,0:T(8,128)(2,1)S(1)}, u32[]{:S(2)}, u32[]{:S(2)}) collective-permute-start(bf16[512,128]{1,0:T(8,128)(2,1)S(1)} %get-tuple-element.49.tab_ref), channel_id=1, source_target_pairs={{0,1},{1,0},{2,3},{3,2},{4,5},{5,4},{6,7},{7,6},{8,9},{9,8},{10,11... | collective-permute-start | bytes 393224 | tf_op jit(solution)/shard_map/ppermute | solution.py:451
  64.5 14.9 %all-to-all-start.2 = ((bf16[16,16,128]{2,1,0:T(8,128)(2,1)}), bf16[16,16,128]{2,1,0:T(8,128)(2,1)S(1)}, u32[]{:S(2)}, u32[]{:S(2)}) async-start(bf16[16,16,128]{2,1,0:T(8,128)(2,1)} %get-tuple-element.50), calls=%async_computation.2 | async-start | bytes 131072 | tf_op jit(solution)/shard_map/all_to_all | solution.py:460
  71.9 11.3 %collective-permute-start.1 = (bf16[2,192,192]{2,1,0:T(8,128)(2,1)S(1)}, bf16[2,192,192]{2,1,0:T(8,128)(2,1)S(1)}, u32[]{:S(2)}, u32[]{:S(2)}) collective-permute-start(bf16[2,192,192]{2,1,0:T(8,128)(2,1)S(1)} %get-tuple-element.45), channel_id=1, source_target_pairs={{0,16},{16,32},{32,48},{48,64},{64,80},{80,96},{96,112},{112,128},... | collective-permute-start | bytes 442376 | tf_op jit(solution)/shard_map/ppermute | solution.py:452
  79.4 10.9 %all-to-all-start.3 = ((bf16[16,32,128]{2,1,0:T(8,128)(2,1)}), bf16[16,32,128]{2,1,0:T(8,128)(2,1)S(1)}, u32[]{:S(2)}, u32[]{:S(2)}) async-start(bf16[16,32,128]{2,1,0:T(8,128)(2,1)} %get-tuple-element.51), calls=%async_computation.3 | async-start | bytes 262144 | tf_op jit(solution)/shard_map/all_to_all | solution.py:461
where the time goes:
time: 92.1 us; the launch traced here: 91.4 us
  starting transfers between devices  30.2 us (33%)
  waiting for transfers between devices  22.3 us (24%)
  Pallas kernels  17.9 us (19%)
  blocking collectives  10.1 us (11%)
  local copies, waits for them, and re-layouts  8.89 us (10%)
  other arithmetic  1.14 us (1%)
    pallas_call x6, Pallas kernels, go(): return run(*kept)  17.9 us
    all_to_all x1, blocking collectives, on_device(): lax.all_to_all(merged, 'lon', split_axis=0, concat_axis=0, tiled=True)  10.1 us
    ppermute x1, waiting for transfers between devices, on_device(): twin = lax.ppermute(tab, 'ens', [(0, 1), (1, 0)])  8.76 us
    all_to_all x1, starting transfers between devices, on_device(): lax.all_to_all(part, ('y', 'core', 'ens'), split_axis=0, concat_axis=0, t...  7.43 us
    ppermute x1, starting transfers between devices, on_device(): halo = lax.ppermute(edge, 'lon', [(k, (k - 1) % 16) for k in range(16)])  7.4 us
    unnamed x46, local copies, waits for them, and re-layouts  6.83 us
    all_to_all x1, starting transfers between devices, on_device(): lax.all_to_all(joined, ('y', 'ens'), split_axis=0, concat_axis=0, tiled=T...  6.35 us
    all_to_all x1, waiting for transfers between devices, on_device(): lax.all_to_all(part, ('y', 'core', 'ens'), split_axis=0, concat_axis=0, t...  6.01 us
  transfers between devices with their start and end apart: 7, of which 4 were waited for; matrix products, arithmetic and copies ran while one was open for 1% of the time, Pallas kernels for 2%

commit v1 on v0

--- a/solution.py
+++ b/solution.py
@@ -2,7 +2,6 @@
 
 import jax
 import jax.numpy as jnp
-import numpy as np
 from jax import lax
 from jax.experimental import pallas as pl
 from jax.experimental.pallas import tpu as pltpu
@@ -12,7 +11,6 @@
 C = 192
 HEADS = 6
 FF = 768
-WO = 12
 ROWS = 144
 LANES = 896
 HX = 72
@@ -24,7 +22,7 @@
 FACTOR = 1.0 / math.sqrt(147456)
 GELU_A = 0.044715
 GELU_C = math.sqrt(2.0 / math.pi)
-PART = 128
+PART = 112
 SLOT = 32
 
 
@@ -40,56 +38,70 @@
     return lax.dot_general(a, b, (((0,), (0,)), ((), ())), preferred_element_type=F32)
 
 
-def token_spread():
-    out = np.zeros((ROWS, LANES), np.float32)
-    for i in range(WO):
-        for h in range(HEADS):
-            for x in range(WO):
-                out[12 * x + i, HX * i + 12 * h + x] = 1.0
-    return out
-
-
-def head_mask():
-    out = np.zeros((C, LANES), np.float32)
-    for lane in range(12 * HX):
-        h = (lane % HX) // 12
-        out[32 * h : 32 * h + 32, lane] = 1.0
-    return out
-
-
-def lag_select():
-    out = np.zeros((12 * ROWS, TAB), np.float32)
+def iota(dims, axis):
+    return lax.broadcasted_iota(jnp.int32, dims, axis).astype(F32)
+
+
+def whole(value, size):
+    return jnp.floor((value + 0.5) * (1.0 / size))
+
+
+def one_hot(hit):
+    return jnp.where(hit, 1.0, 0.0).astype(BF16)
+
+
+def prep_kernel(qkv_hbm, proj_hbm, fc1_hbm, fc2_hbm, tab_hbm,
+                wt_ref, projb_ref, fc1b_ref, fc2b_ref, bias_ref, spread_ref, mask_ref, sel_ref,
+                ra_ref, ca_ref, rb_ref, cb_ref,
+                qkv_ref, proj_ref, fc1_ref, fc2_ref, tab_ref, sems):
+    copies = [
+        pltpu.make_async_copy(src, dst, sems.at[k])
+        for k, (src, dst) in enumerate(
+            ((tab_hbm, tab_ref), (qkv_hbm, qkv_ref), (proj_hbm, proj_ref), (fc1_hbm, fc1_ref),
+             (fc2_hbm, fc2_ref))
+        )
+    ]
+    for copy in copies:
+        copy.start()
+    lane = iota((8, LANES), 1)
+    cell = whole(lane, HX)
+    rest = lane - HX * cell
+    head = whole(rest, 12)
+    token = 12.0 * (rest - 12.0 * head) + cell
+    token = jnp.where(lane < 12.0 * HX, token, -1.0)[0:1]
+    head = jnp.where(lane < 12.0 * HX, head, -1.0)[0:1]
+    spread_ref[...] = one_hot(iota((ROWS, LANES), 0) == token)
+    for h in range(HEADS):
+        mask_ref[32 * h : 32 * h + 32, :] = one_hot(
+            jnp.broadcast_to(head, (32, LANES)) == float(h)
+        )
+    row = iota((ROWS, 128), 0)
+    level = whole(row, 12)
+    base = 44.0 * level - row + 11.0
+    column_id = iota((ROWS, 128), 1)
     for i in range(12):
-        for y in range(12):
-            for j in range(12):
-                out[i * ROWS + 12 * y + j, 32 * y + i - j + 11] = 1.0
-    return out
-
-
-def bias_places():
-    rows_a = np.zeros((16, 1344), np.float32)
-    cols_a = np.zeros((1344, 128), np.float32)
-    rows_b = np.zeros((16, 1152), np.float32)
-    cols_b = np.zeros((1152, 128), np.float32)
-    for n in range(576):
-        rows_a[n // 36, n] = 1.0
-        cols_a[n, n % 36] = 1.0
-    for n in range(768):
-        rows_a[n // 48, 576 + n] = 1.0
-        cols_a[576 + n, 36 + n % 48] = 1.0
+        for t in range(3):
+            sel_ref[ROWS * i : ROWS * i + ROWS, 128 * t : 128 * t + 128] = one_hot(
+                base + float(i) == column_id + 128.0 * t
+            )
+    n = iota((576, 128), 0)
+    spot = iota((576, 128), 1)
+    ca_ref[0:576, :] = one_hot(spot == n - 36.0 * whole(n, 36))
+    n = iota((768, 128), 0)
+    spot = iota((768, 128), 1)
+    ca_ref[576:1344, :] = one_hot(spot == n - 48.0 * whole(n, 48) + 36.0)
+    n = iota((192, 128), 0)
+    spot = iota((192, 128), 1)
+    n = n - 12.0 * whole(n, 12)
     for k in range(6):
-        for n in range(192):
-            rows_b[n // 12, 192 * k + n] = 1.0
-            cols_b[192 * k + n, 12 * k + n % 12] = 1.0
-    return rows_a, cols_a, rows_b, cols_b
-
-
-def prep_kernel(qkv_ref, proj_ref, fc1_ref, fc2_ref, tab_ref, sel_ref,
-                wt_ref, projb_ref, fc1b_ref, fc2b_ref, bias_ref):
-    wt_ref[...] = qkv_ref[...].T.astype(BF16)
-    projb_ref[...] = proj_ref[...].astype(BF16)
-    fc1b_ref[...] = fc1_ref[...].astype(BF16)
-    fc2b_ref[...] = fc2_ref[...].astype(BF16)
+        cb_ref[192 * k : 192 * k + 192, :] = one_hot(spot == n + 12.0 * k)
+    n = iota((16, 1344), 1)
+    n = jnp.where(n < 576.0, whole(n, 36), whole(n - 576.0, 48))
+    ra_ref[...] = one_hot(n == iota((16, 1344), 0))
+    n = iota((16, 1152), 1)
+    n = whole(n - 192.0 * whole(n, 192), 12)
+    rb_ref[...] = one_hot(n == iota((16, 1152), 0))
+    copies[0].wait()
     tiles = []
     for t in range(3):
         tile = None
@@ -112,6 +124,14 @@
     for v in range(2):
         spare = jnp.zeros((ROWS, LANES - 12 * HX), F32)
         bias_ref[v] = jnp.concatenate(pieces[v] + [spare], axis=1)
+    copies[1].wait()
+    wt_ref[...] = qkv_ref[...].T.astype(BF16)
+    copies[2].wait()
+    projb_ref[...] = proj_ref[...].astype(BF16)
+    copies[3].wait()
+    fc1b_ref[...] = fc1_ref[...].astype(BF16)
+    copies[4].wait()
+    fc2b_ref[...] = fc2_ref[...].astype(BF16)
 
 
 def column(row):
@@ -165,10 +185,11 @@
     return inverse * (scaled - first - hat * second)
 
 
-def main_kernel(core_ref, x_ref, cot_ref, n1g_ref, n1o_ref, qb_ref, pb_ref, n2g_ref, n2o_ref,
-                f1b_ref, f2b_ref, spread_ref, mask_ref, sel_ref, ra_ref, ca_ref, rb_ref, cb_ref,
-                halo_ref, bias_ref, wt_ref, proj_ref, fc1_ref, fc2_ref,
-                both_ref, edge_ref, own_ref, send_ref, low_ref, sum_ref, stage_ref, tab_ref):
+def front_kernel(x_ref, cot_ref, n1g_ref, n1o_ref, qb_ref, pb_ref, n2g_ref, n2o_ref,
+                 f1b_ref, f2b_ref, halo_ref, bias_ref, wt_ref, proj_ref, fc1_ref, fc2_ref,
+                 spread_ref, mask_ref, sel_ref,
+                 low_ref, block_ref, few_ref, wide_ref, hat_ref, inv_ref, rg_ref, row_ref, f1s_ref,
+                 sum_ref, tab_ref):
     n1g, n1o, qb, pb, n2g, n2o, f1b, f2b = (
         ref[...].reshape(1, -1)
         for ref in (n1g_ref, n1o_ref, qb_ref, pb_ref, n2g_ref, n2o_ref, f1b_ref, f2b_ref)
@@ -232,10 +253,7 @@
     pre_grad = jnp.concatenate(grads, axis=0)
     f1_sum = f1_sums[0] + f1_sums[1] + f1_sums[2] + f1_sums[3]
     block = (resid + nt(activated, fc2_ref[...]) + f2b).astype(BF16)
-    back = natural_picks()
-    placed = nn(back, block).astype(BF16)
-    both_ref[0] = placed[:576]
-    edge_ref[0] = placed[576:]
+    block_ref[...] = block
     n2_grad = nt(pre_grad, fc1_ref[...])
     n2g_sum = jnp.sum(n2_grad * hat2, axis=0, keepdims=True)
     n2o_sum = jnp.sum(n2_grad, axis=0, keepdims=True)
@@ -266,17 +284,6 @@
         key_t = (nt(wk, own) + bk).astype(BF16)
         mixed = (nn(key_t, low) * SCALE).astype(BF16) * mask
         grad_q.append(nt(spread, mixed).astype(BF16))
-    dq = jnp.concatenate(grad_q, axis=0)
-    dk = jnp.concatenate(grad_k, axis=0)
-    dv = jnp.concatenate(grad_v, axis=0)
-    n1_grad = nn(dq, wq) + nn(dk, wk) + nn(dv, wv)
-    n1g_sum = jnp.sum(n1_grad * hat1, axis=0, keepdims=True)
-    n1o_sum = jnp.sum(n1_grad, axis=0, keepdims=True)
-    input_grad = (resid_grad + norm_back(n1_grad, hat1, inv1, n1g)).astype(BF16)
-    placed = nn(back, input_grad).astype(BF16)
-    both_ref[1] = placed[:576]
-    edge_ref[1] = placed[576:]
-    sums = [jnp.sum(d.astype(F32), axis=0, keepdims=True) for d in (dq, dk, dv)]
     for v in range(2):
         turned = sum_ref[v].T
         total = jnp.zeros((HX, TAB), F32)
@@ -287,13 +294,62 @@
             tab_ref[ROWS * t + HX * v : ROWS * t + HX * v + HX, :] = total[:, 128 * t : 128 * t + 128]
     tab_ref[3 * ROWS :, :] = jnp.zeros((16 * SLOT - 3 * ROWS, 128), F32)
     low_ref[...] = tab_ref[...].astype(BF16)
+    for k, group in enumerate((grad_q, grad_k, grad_v)):
+        for g in range(4):
+            few_ref[k, ROWS * g : ROWS * g + ROWS, :] = group[g]
+    few_ref[3] = normed
+    few_ref[4] = normed2
+    few_ref[5] = cot_low
+    few_ref[6] = attn_grad
+    few_ref[7] = attended
+    wide_ref[0] = pre_grad
+    wide_ref[1] = activated
+    hat_ref[...] = hat1
+    inv_ref[...] = inv1
+    rg_ref[...] = resid_grad
+    row_ref[0:1, :] = pb_sum
+    row_ref[1:2, :] = f2_sum
+    row_ref[2:3, :] = n2g_sum
+    row_ref[3:4, :] = n2o_sum
+    f1s_ref[...] = f1_sum
+
+
+def back_kernel(core_ref, n1g_ref, block_ref, few_ref, wide_ref, hat_ref, inv_ref, rg_ref, row_ref,
+                f1s_ref, wt_ref, ra_ref, ca_ref, rb_ref, cb_ref,
+                out_ref, edge_ref, own_ref, send_ref, stage_ref):
+    wq = wt_ref[0:192, :]
+    wk = wt_ref[192:384, :]
+    wv = wt_ref[384:576, :]
+    n1g = n1g_ref[...].reshape(1, -1)
+    dq = few_ref[0]
+    dk = few_ref[1]
+    dv = few_ref[2]
+    normed = few_ref[3]
+    hat1 = hat_ref[...]
+    f1_sum = f1s_ref[...]
+    pb_sum = row_ref[0:1, :]
+    f2_sum = row_ref[1:2, :]
+    n2g_sum = row_ref[2:3, :]
+    n2o_sum = row_ref[3:4, :]
+    back = natural_picks()
+    placed = nn(back, block_ref[...]).astype(BF16)
+    out_ref[0] = placed[:576]
+    edge_ref[0] = placed[576:]
+    n1_grad = nn(dq, wq) + nn(dk, wk) + nn(dv, wv)
+    n1g_sum = jnp.sum(n1_grad * hat1, axis=0, keepdims=True)
+    n1o_sum = jnp.sum(n1_grad, axis=0, keepdims=True)
+    input_grad = (rg_ref[...] + norm_back(n1_grad, hat1, inv_ref[...], n1g)).astype(BF16)
+    placed = nn(back, input_grad).astype(BF16)
+    out_ref[1] = placed[:576]
+    edge_ref[1] = placed[576:]
+    sums = [jnp.sum(d.astype(F32), axis=0, keepdims=True) for d in (dq, dk, dv)]
     dw_q = tn(dq, normed)
     dw_k = tn(dk, normed)
     dw_v = tn(dv, normed)
     dw_qkv = jnp.concatenate([dw_q, dw_k, dw_v], axis=0)
-    dw_p = tn(attn_grad, attended)
-    dw_1 = tn(pre_grad, normed2)
-    dw_2 = tn(cot_low, activated)
+    dw_p = tn(few_ref[6], few_ref[7])
+    dw_1 = tn(wide_ref[0], few_ref[4])
+    dw_2 = tn(few_ref[5], wide_ref[1])
     vec_a = jnp.concatenate(sums + [f1_sum[:, 0:192], f1_sum[:, 192:384], f1_sum[:, 384:576], f1_sum[:, 576:768]], axis=1)
     vec_b = jnp.concatenate([pb_sum, f2_sum, n1g_sum, n1o_sum, n2g_sum, n2o_sum], axis=1)
     row_a = nn((ra_ref[...].astype(F32) * vec_a).astype(BF16), ca_ref[...])
@@ -309,38 +365,24 @@
         a_rest = jnp.concatenate([a36[:, 128:], a12[:, 128:]], axis=0)
         stage_ref[0, top + 48 : top + 96, :] = jnp.concatenate([a_rest, b48[:, 128:]], axis=1)
         stage_ref[0, top + 96 : top + 108, :] = d12[:, 640:]
-        stage_ref[0, top + 108 : top + 112, :] = jnp.zeros((4, 128), F32)
-        stage_ref[0, top + 112 : top + 128, :] = jnp.concatenate(
-            [row_a[l : l + 1], row_b[l : l + 1], jnp.zeros((14, 128), F32)], axis=0
-        )
+        stage_ref[0, top + 108 : top + 109, :] = row_a[l : l + 1]
+        stage_ref[0, top + 109 : top + 110, :] = row_b[l : l + 1]
+        stage_ref[0, top + 110 : top + 112, :] = jnp.zeros((2, 128), F32)
         stage_ref[1, top : top + 48, :] = b48[:, :128]
         for b in range(5):
-            piece = d12[:, 128 * b : 128 * b + 128]
-            stage_ref[1, top + 48 + 16 * b : top + 64 + 16 * b, :] = jnp.concatenate(
-                [piece, jnp.zeros((4, 128), F32)], axis=0
-            )
+            stage_ref[1, top + 48 + 12 * b : top + 60 + 12 * b, :] = d12[:, 128 * b : 128 * b + 128]
+        stage_ref[1, top + 108 : top + 112, :] = jnp.zeros((4, 128), F32)
     core = core_ref[0]
-    for k in range(8):
-        for l in range(16):
-            rows = slice(PART * l + 16 * k, PART * l + 16 * k + 16)
-            spot = slice(16 * l, 16 * l + 16)
-            own_ref[k, spot, :] = stage_ref[core, rows, :].astype(BF16)
-            send_ref[k, spot, :] = stage_ref[1 - core, rows, :].astype(BF16)
-
-
-def join_kernel(own_ref, got_ref, out_ref):
-    out_ref[...] = (own_ref[...].astype(F32) + got_ref[...].astype(F32)).astype(BF16)
-
-
-def band_sum_kernel(in_ref, tab_ref, twin_ref, out_ref):
-    total = in_ref[0].astype(F32)
-    for k in range(1, 8):
-        total = total + in_ref[k].astype(F32)
-    low = total.astype(BF16)
-    table = (tab_ref[...].astype(F32) + twin_ref[...].astype(F32)).astype(BF16)
+    own_ref[...] = stage_ref[core].astype(BF16)
+    send_ref[...] = stage_ref[1 - core].astype(BF16)
+
+
+def join_kernel(own_ref, got_ref, tab_ref, twin_ref, out_ref):
     for l in range(16):
-        out_ref[l, 0:16, :] = low[16 * l : 16 * l + 16]
-        out_ref[l, 16:, :] = table[SLOT * l : SLOT * l + SLOT]
+        part = slice(PART * l, PART * l + PART)
+        out_ref[l, 0:PART, :] = (own_ref[part].astype(F32) + got_ref[part].astype(F32)).astype(BF16)
+        spot = slice(SLOT * l, SLOT * l + SLOT)
+        out_ref[l, PART:, :] = (tab_ref[spot].astype(F32) + twin_ref[spot].astype(F32)).astype(BF16)
 
 
 def lon_sum_kernel(in_ref, part_ref, tab_ref):
@@ -348,31 +390,44 @@
     for l in range(1, 16):
         total = total + in_ref[l].astype(F32)
     low = total.astype(BF16)
+    part_ref[...] = low[:PART]
     for k in range(16):
-        part_ref[k] = low[:16]
-        tab_ref[k] = low[16:]
-
-
-def final_kernel(part_ref, tab_ref, qw_ref, pw_ref, f1_ref, f2_ref, qb_ref, pb_ref, f1b_ref, f2b_ref,
-                 n1g_ref, n1o_ref, n2g_ref, n2o_ref, out_tab_ref):
-    def half(core):
-        rows = [part_ref[4 * y + 2 * core + e] for y in range(4) for e in range(2)]
-        return jnp.concatenate(rows, axis=0).astype(F32) * FACTOR
-
-    first = half(0)
-    second = half(1)
+        tab_ref[k] = low[PART:]
+
+
+def band_sum_kernel(slot_ref, *refs):
+    out_ref, all_ref = refs[8], refs[9]
+    slot = slot_ref[0]
+    for k in range(8):
+        all_ref[jnp.bitwise_xor(slot, k)] = refs[k][...].astype(F32)
+    total = all_ref[0]
+    for k in range(1, 8):
+        total = total + all_ref[k]
+    out_ref[...] = total.astype(BF16)
+
+
+def weight_kernel(core_ref, own_ref, got_ref, qw_ref, pw_ref, f1_ref, f2_ref, qb_ref, pb_ref, f1b_ref,
+                  f2b_ref, n1g_ref, n1o_ref, n2g_ref, n2o_ref, pair_ref):
+    core = core_ref[0]
+    pair_ref[core] = own_ref[...].astype(F32) * FACTOR
+    pair_ref[1 - core] = got_ref[...].astype(F32) * FACTOR
+    first = pair_ref[0]
+    second = pair_ref[1]
     a = jnp.concatenate([first[0:48], first[48:96, 0:64]], axis=1)
     qw_ref[...] = a[0:36]
     pw_ref[...] = a[36:48]
     f1_ref[...] = jnp.concatenate([second[0:48], first[48:96, 64:128]], axis=1)
-    d = [second[48 + 16 * k : 60 + 16 * k] for k in range(5)] + [first[96:108]]
+    d = [second[48 + 12 * k : 60 + 12 * k] for k in range(5)] + [first[96:108]]
     f2_ref[...] = jnp.concatenate(d, axis=1)
-    va = first[112:113]
-    vb = first[113:114]
+    va = first[108:109]
+    vb = first[109:110]
     qb_ref[...] = va[:, 0:36].reshape(36)
     f1b_ref[...] = va[:, 36:84].reshape(48)
     for k, ref in enumerate((pb_ref, f2b_ref, n1g_ref, n1o_ref, n2g_ref, n2o_ref)):
         ref[...] = vb[:, 12 * k : 12 * k + 12].reshape(12)
+
+
+def table_kernel(tab_ref, out_tab_ref):
     tab = tab_ref[...].astype(F32)
     for t in range(3):
         tile = tab[ROWS * t : ROWS * t + ROWS]
@@ -381,10 +436,11 @@
             out_tab_ref[pl.ds(4 * t + k, ROWS, stride=12), :] = piece[:, :23]
 
 
-def call(kernel, out_shape, smem=0, far=0, near=0, limit=8, scratch=()):
+def call(kernel, out_shape, smem=0, far=0, near=0, limit=8, scratch=(), raw=False, flops=0):
     count = smem + far + near
+    space = pltpu.HBM if raw else pltpu.VMEM
     specs = [pl.BlockSpec(memory_space=pltpu.SMEM)] * smem + [
-        pl.BlockSpec(memory_space=pltpu.VMEM)
+        pl.BlockSpec(memory_space=space)
     ] * (far + near)
     run = pl.pallas_call(
         kernel,
@@ -393,9 +449,14 @@
         out_specs=jax.tree.map(lambda _: pl.BlockSpec(memory_space=pltpu.VMEM), out_shape),
         scratch_shapes=scratch,
         compiler_params=pltpu.CompilerParams(vmem_limit_bytes=limit << 20),
+        cost_estimate=pl.CostEstimate(flops=flops, transcendentals=0, bytes_accessed=0)
+        if flops
+        else None,
     )
 
     def go(*args):
+        if raw:
+            args = tuple(pltpu.with_memory_space_constraint(a, pltpu.HBM) for a in args)
         kept = args[: smem + far] + tuple(
             pltpu.with_memory_space_constraint(a, pltpu.VMEM) for a in args[smem + far :]
         )
@@ -421,51 +482,71 @@
     cot = cotangent.reshape(576, C)
     edge = jnp.stack([inputs[0, :, :, :8, :].reshape(192, C), cotangent[0, :, :, :8, :].reshape(192, C)])
     halo = lax.ppermute(edge, "lon", [(k, (k - 1) % 16) for k in range(16)])
-    spread = jnp.asarray(token_spread(), BF16)
-    mask = jnp.asarray(head_mask(), BF16)
-    sel = jnp.asarray(lag_select(), BF16)
-    ra, ca, rb, cb = (jnp.asarray(a, BF16) for a in bias_places())
     table = bias_table.reshape(12 * ROWS, 23)
-    wt, proj, fc1, fc2, bias = call(
+    wt, proj, fc1, fc2, bias, spread, mask, sel, ra, ca, rb, cb = call(
         prep_kernel,
         [near((576, C), BF16), near((C, C), BF16), near((C, FF), BF16), near((C, FF), BF16),
-         near((2, ROWS, LANES), F32)],
-        far=6,
+         near((2, ROWS, LANES), F32), near((ROWS, LANES), BF16), near((C, LANES), BF16),
+         near((12 * ROWS, TAB), BF16), near((16, 1344), BF16), near((1344, 128), BF16),
+         near((16, 1152), BF16), near((1152, 128), BF16)],
+        far=5,
         limit=16,
-    )(qkv_weight, proj_weight, fc1_weight, fc2_weight.T, table, sel)
+        raw=True,
+        scratch=[pltpu.VMEM((C, 576), F32), pltpu.VMEM((C, C), F32), pltpu.VMEM((C, FF), F32),
+                 pltpu.VMEM((C, FF), F32), pltpu.VMEM((12 * ROWS, 23), F32),
+                 pltpu.SemaphoreType.DMA((5,))],
+    )(qkv_weight, proj_weight, fc1_weight, fc2_weight.T, table)
     core = lax.axis_index("core").astype(jnp.int32).reshape(1)
-    both, ends, own, send, tab = call(
-        main_kernel,
-        [shape((2, 576, C), BF16), near((2, 192, C), BF16), near((8, 256, 128), BF16),
-         near((8, 256, 128), BF16), near((16 * SLOT, 128), BF16)],
+    slot = (2 * lax.axis_index("y") + lax.axis_index("ens")).astype(jnp.int32).reshape(1)
+    tab, *state = call(
+        front_kernel,
+        [near((16 * SLOT, 128), BF16), near((576, C), BF16), near((8, 576, C), BF16),
+         near((2, 576, FF), BF16), near((576, C), F32), near((576, 1), F32), near((576, C), F32),
+         near((8, C), F32), near((1, FF), F32)],
+        far=10,
+        near=9,
+        limit=24,
+        scratch=[pltpu.VMEM((2, ROWS, LANES), F32), pltpu.VMEM((16 * SLOT, 128), F32)],
+    )(x, cot, norm1_gain, norm1_offset, qkv_bias, proj_bias, norm2_gain, norm2_offset, fc1_bias,
+      fc2_bias, halo, bias, wt, proj, fc1, fc2, spread, mask, sel)
+    twin = lax.ppermute(tab, "ens", [(0, 1), (1, 0)])
+    both, ends, own, send = call(
+        back_kernel,
+        [shape((2, 576, C), BF16), near((2, 192, C), BF16), near((16 * PART, 128), BF16),
+         near((16 * PART, 128), BF16)],
         smem=1,
-        far=17,
-        near=6,
-        limit=36,
-        scratch=[pltpu.VMEM((2, ROWS, LANES), F32), pltpu.VMEM((2, 16 * PART, 128), F32),
-                 pltpu.VMEM((16 * SLOT, 128), F32)],
-    )(core, x, cot, norm1_gain, norm1_offset, qkv_bias, proj_bias,
-      norm2_gain, norm2_offset, fc1_bias, fc2_bias, spread, mask, sel, ra, ca, rb, cb,
-      halo, bias, wt, proj, fc1, fc2)
+        far=1,
+        near=13,
+        limit=16,
+        scratch=[pltpu.VMEM((2, 16 * PART, 128), F32)],
+    )(core, norm1_gain, *state, wt, ra, ca, rb, cb)
     got = lax.ppermute(send, "core", [(0, 1), (1, 0)])
-    twin = lax.ppermute(tab, "ens", [(0, 1), (1, 0)])
     home = lax.ppermute(ends, "lon", [(k, (k + 1) % 16) for k in range(16)])
-    joined = call(join_kernel, near((8, 256, 128), BF16), near=2)(own, got)
-    bands = lax.all_to_all(joined, ("y", "ens"), split_axis=0, concat_axis=0, tiled=True)
-    merged = call(band_sum_kernel, near((16, 16 + SLOT, 128), BF16), near=3)(bands, tab, twin)
-    arrived = lax.all_to_all(merged, "lon", split_axis=0, concat_axis=0, tiled=True)
+    joined = call(join_kernel, near((16, PART + SLOT, 128), BF16), near=4)(own, got, tab, twin)
+    arrived = lax.all_to_all(joined, "lon", split_axis=0, concat_axis=0, tiled=True)
     part, tab_copies = call(
-        lon_sum_kernel, [near((16, 16, 128), BF16), near((16, SLOT, 128), BF16)], near=1
+        lon_sum_kernel, [near((PART, 128), BF16), near((16, SLOT, 128), BF16)], near=1
     )(arrived)
-    parts = lax.all_to_all(part, ("y", "core", "ens"), split_axis=0, concat_axis=0, tiled=True)
+    bands = [part] + [
+        lax.ppermute(part, ("y", "ens"), [(n, n ^ k) for n in range(8)]) for k in range(1, 8)
+    ]
     tab_all = lax.all_to_all(tab_copies, "lon", split_axis=0, concat_axis=0, tiled=True)
-    qw, pw, f1, f2, qb, pb, f1b, f2b, n1g, n1o, n2g, n2o, tab_out = call(
-        final_kernel,
+    half = call(
+        band_sum_kernel, near((PART, 128), BF16), smem=1, near=8,
+        scratch=[pltpu.VMEM((8, PART, 128), F32)],
+    )(slot, *bands)
+    other = lax.ppermute(half, "core", [(0, 1), (1, 0)])
+    qw, pw, f1, f2, qb, pb, f1b, f2b, n1g, n1o, n2g, n2o = call(
+        weight_kernel,
         [shape((36, C), F32), shape((12, C), F32), shape((48, C), F32), shape((12, FF), F32),
-         shape((36,), F32), shape((12,), F32), shape((48,), F32)] + [shape((12,), F32)] * 5
-        + [shape((12 * ROWS, 23), F32)],
+         shape((36,), F32), shape((12,), F32), shape((48,), F32)] + [shape((12,), F32)] * 5,
+        smem=1,
         near=2,
-    )(parts, tab_all.reshape(16 * SLOT, 128))
+        scratch=[pltpu.VMEM((2, PART, 128), F32)],
+    )(core, half, other)
+    tab_out = call(table_kernel, shape((12 * ROWS, 23), F32), near=1)(
+        tab_all.reshape(16 * SLOT, 128)
+    )
     full = both.reshape(2, *grid[1:])
     ends = home.reshape(2, grid[1], grid[2], 8, C)[:, :, :, :6]
     full = jnp.concatenate([ends, full[:, :, :, 6:]], axis=3)

time: 92.1 us -> 88.8 us (0.964)
  starting transfers between devices: 30.2 us -> 44.2 us
  blocking collectives: 10.1 us -> 0 us
  local copies, waits for them, and re-layouts: 8.89 us -> 2.16 us
  waiting for transfers between devices: 22.3 us -> 20.1 us
  Pallas kernels: 17.9 us -> 20 us
    ppermute x0 -> x8, starting transfers between devices: none -> 19.4 us  [the longest x7 14.3 us: on_device(): lax.ppermute(part, ('y', 'ens'), [(n, n ^ k) for n in range(8)])]
    all_to_all x1 -> x0, blocking collectives: 10.1 us -> none  [on_device(): lax.all_to_all(merged, 'lon', split_axis=0, concat_axis=0, tiled=True)]
    all_to_all x2 -> x1, starting transfers between devices: 13.8 us -> 5.71 us  [on_device(): lax.all_to_all(joined, 'lon', split_axis=0, concat_axis=0, tiled=True)]
    all_to_all x2 -> x1, waiting for transfers between devices: 6.02 us -> 13.6 us  [on_device(): lax.all_to_all(joined, 'lon', split_axis=0, concat_axis=0, tiled=True)]
    unnamed x46 -> x20, local copies, waits for them, and re-layouts: 6.83 us -> 0.04 us
    all_to_all x1, waiting for transfers between devices: 6 us -> 0.01 us  [on_device(): lax.all_to_all(tab_copies, 'lon', split_axis=0, concat_axis=0, tiled=True)]
    ppermute x1, waiting for transfers between devices: 8.76 us -> 4.01 us  [on_device(): twin = lax.ppermute(tab, 'ens', [(0, 1), (1, 0)])]
    all_to_all x1, starting transfers between devices: 3.52 us -> 6.28 us  [on_device(): lax.all_to_all(tab_copies, 'lon', split_axis=0, concat_axis=0, tiled=True)]
  transfers between devices with their start and end apart: 7 -> 14, of which waited for: 4 -> 5; matrix products, arithmetic and copies ran while one was open for 1% -> 2% of each run, Pallas kernels for 2% -> 5%
where the time goes in v1:
time: 88.8 us; the launch traced here: 88.5 us
  starting transfers between devices  44.2 us (50%)
  waiting for transfers between devices  20.1 us (23%)
  Pallas kernels  20 us (23%)
  local copies, waits for them, and re-layouts  2.16 us (2%)
  other arithmetic  1.14 us (1%)
    pallas_call x8, Pallas kernels, go(): return run(*kept)  20 us
    ppermute x7, starting transfers between devices, on_device(): lax.ppermute(part, ('y', 'ens'), [(n, n ^ k) for n in range(8)])  14.3 us
    all_to_all x1, waiting for transfers between devices, on_device(): lax.all_to_all(joined, 'lon', split_axis=0, concat_axis=0, tiled=True)  13.6 us
    ppermute x1, starting transfers between devices, on_device(): halo = lax.ppermute(edge, 'lon', [(k, (k - 1) % 16) for k in range(16)])  7.4 us
    all_to_all x1, starting transfers between devices, on_device(): lax.all_to_all(tab_copies, 'lon', split_axis=0, concat_axis=0, tiled=True)  6.28 us
    all_to_all x1, starting transfers between devices, on_device(): lax.all_to_all(joined, 'lon', split_axis=0, concat_axis=0, tiled=True)  5.71 us
    ppermute x1, starting transfers between devices, on_device(): other = lax.ppermute(half, 'core', [(0, 1), (1, 0)])  5.05 us
    ppermute x1, waiting for transfers between devices, on_device(): twin = lax.ppermute(tab, 'ens', [(0, 1), (1, 0)])  4.01 us
  transfers between devices with their start and end apart: 14, of which 5 were waited for; matrix products, arithmetic and copies ran while one was open for 2% of the time, Pallas kernels for 5%

profile of v1, /device:TPU:1, one launch (start us, length us, event | category | flops | bytes accessed | tf_op | source)
XLA Modules:
  0.0 88.5 jit_solution(8416100204358327770)
XLA Ops:
  0.6 0.0 copy-start
  0.7 0.0 copy-start.1
  0.7 0.0 copy-start.2
  0.7 0.0 copy-start.5
  0.7 0.0 copy-start.3
  0.7 0.0 copy-start.6
  0.7 0.0 copy-start.7
  0.7 0.0 copy-start.8
  0.7 0.0 copy-start.4
  0.7 0.0 copy-start.9
  0.8 1.0 %slice.18 = bf16[1,4,6,8,192]{4,3,2,1,0:T(8,128)(2,1)S(1)} slice(bf16[1,4,6,24,192]{4,3,2,1,0:T(8,128)(2,1)} %param.15), slice={[0:1], [0:4], [0:6], [0:8], [0:192]} | slice | bytes 147456 | tf_op jit(solution)/shard_map/slice | solution.py:483
  1.7 0.9 %slice.19 = bf16[1,4,6,8,192]{4,3,2,1,0:T(8,128)(2,1)S(1)} slice(bf16[1,4,6,24,192]{4,3,2,1,0:T(8,128)(2,1)} %param.16), slice={[0:1], [0:4], [0:6], [0:8], [0:192]} | slice | bytes 147456 | tf_op jit(solution)/shard_map/slice | solution.py:483
  2.6 7.4 %collective-permute-start = (bf16[2,192,192]{2,1,0:T(8,128)(2,1)S(1)}, bf16[2,192,192]{2,1,0:T(8,128)(2,1)S(1)}, u32[]{:S(2)}, u32[]{:S(2)}) collective-permute-start(bf16[2,192,192]{2,1,0:T(8,128)(2,1)S(1)} %pad_maximum_fusion.1), channel_id=1, source_target_pairs={{0,240},{16,0},{32,16},{48,32},{64,48},{80,64},{96,80},{112,96},{1... | collective-permute-start | bytes 442376 | tf_op jit(solution)/shard_map/ppermute | solution.py:484
  10.0 2.9 %shard_map.262 = (bf16[576,192]{1,0:T(8,128)(2,1)S(1)}, bf16[192,192]{1,0:T(8,128)(2,1)S(1)}, bf16[192,768]{1,0:T(8,128)(2,1)S(1)}, bf16[192,768]{1,0:T(8,128)(2...) custom-call(f32[192,576]{1,0:T(8,128)} %qkv_hbm.1, ...), custom_call_target="tpu_custom_call" | custom-call | tf_op jit(solution)/shard_map/pallas_call | solution.py:464
  12.9 0.7 collective-permute-done.halo_ref
  13.6 0.0 copy-done
  13.6 0.0 copy-done.1
  13.6 0.0 copy-done.2
  13.6 0.0 copy-done.5
  13.6 0.0 copy-done.3
  13.6 0.0 copy-done.6
  13.7 0.0 copy-done.7
  13.7 0.0 copy-done.8
  13.7 0.0 copy-done.4
  13.7 0.0 copy-done.9
  13.7 11.0 %shard_map.263 = (bf16[512,128]{1,0:T(8,128)(2,1)S(1)}, bf16[576,192]{1,0:T(8,128)(2,1)S(1)}, bf16[8,576,192]{2,1,0:T(8,128)(2,1)S(1)}, bf16[2,576,768]{2,1,0:T(...) custom-call(bf16[576,192]{1,0:T(8,128)(2,1)S(1)} %bitcast.18, ...), custom_call_target="tpu_custom_call" | custom-call | tf_op jit(solution)/shard_map/pallas_call | solution.py:464
  24.7 2.7 %shard_map.264 = (bf16[2,576,192]{2,1,0:T(8,128)(2,1)S(1)}, bf16[2,192,192]{2,1,0:T(8,128)(2,1)S(1)}, bf16[1792,128]{1,0:T(8,128)(2,1)S(1)}, bf16[1792,128]{1,0:T(8,128)(2,1)S(1)}) custom-call(s32[1]{0:T(128)} %bitcast.core_ref, f32[192]{0:T(256)S(1)} %copy-done.2, bf16[576,192]{1,0:T(8,128)(2,1)S(1)} %get-tuple-element.62.block_ref, ...), custom_call_target="tpu_custom_call" | custom-call | tf_op jit(solution)/shard_map/pallas_call | solution.py:464
  27.3 1.6 %collective-permute-start.2 = (bf16[1792,128]{1,0:T(8,128)(2,1)S(1)}, bf16[1792,128]{1,0:T(8,128)(2,1)S(1)}, u32[]{:S(2)}, u32[]{:S(2)}) collective-permute-start(bf16[1792,128]{1,0:T(8,128)(2,1)S(1)} %get-tuple-element.77), channel_id=1, source_target_pairs={{0,2},{2,0},{1,3},{3,1},{4,6},{6,4},{5,7},{7,5},{8,10},{10,8},{9,1... | collective-permute-start | bytes 1376264 | tf_op jit(solution)/shard_map/ppermute | solution.py:523
  28.9 2.4 %collective-permute-start.3 = (bf16[512,128]{1,0:T(8,128)(2,1)S(1)}, bf16[512,128]{1,0:T(8,128)(2,1)S(1)}, u32[]{:S(2)}, u32[]{:S(2)}) collective-permute-start(bf16[512,128]{1,0:T(8,128)(2,1)S(1)} %get-tuple-element.78.tab_ref), channel_id=1, source_target_pairs={{0,1},{1,0},{2,3},{3,2},{4,5},{5,4},{6,7},{7,6},{8,9},{9,8},{10,11... | collective-permute-start | bytes 393224 | tf_op jit(solution)/shard_map/ppermute | solution.py:512
  31.4 4.0 %collective-permute-done.3.twin_ref = bf16[512,128]{1,0:T(8,128)(2,1)S(1)} collective-permute-done((bf16[512,128]{1,0:T(8,128)(2,1)S(1)}, bf16[512,128]{1,0:T(8,128)(2,1)S(1)}, u32[]{:S(2)}, u32[]{:S(2)}) %collective-permute-start.3) | collective-permute-done | bytes 131104 | tf_op jit(solution)/shard_map/ppermute | solution.py:512
  35.4 0.0 collective-permute-done.2.got_ref
  35.4 1.0 %shard_map.265 = bf16[16,144,128]{2,1,0:T(8,128)(2,1)} custom-call(bf16[1792,128]{1,0:T(8,128)(2,1)S(1)} %get-tuple-element.76.own_ref, bf16[1792,128]{1,0:T(8,128)(2,1)S(1)} %collective-permute-done.2.got_ref, bf16[512,128]{1,0:T(8,128)(2,1)S(1)} %get-tuple-element.78.tab_ref, bf16[512,128]{1,0:T(8,128)(2,1)S(1)} %collective-permute-done.3.twin_ref), custom_call_target="tpu_custom_call" | custom-call | tf_op jit(solution)/shard_map/pallas_call | solution.py:464
  36.4 5.7 %all-to-all-start = ((bf16[16,144,128]{2,1,0:T(8,128)(2,1)}), bf16[16,144,128]{2,1,0:T(8,128)(2,1)S(1)}, u32[]{:S(2)}, u32[]{:S(2)}) async-start(bf16[16,144,128]{2,1,0:T(8,128)(2,1)} %shard_map.265), calls=%async_computation | async-start | bytes 1179648 | tf_op jit(solution)/shard_map/all_to_all | solution.py:526
  42.1 1.4 %collective-permute-start.1 = (bf16[2,192,192]{2,1,0:T(8,128)(2,1)S(1)}, bf16[2,192,192]{2,1,0:T(8,128)(2,1)S(1)}, u32[]{:S(2)}, u32[]{:S(2)}) collective-permute-start(bf16[2,192,192]{2,1,0:T(8,128)(2,1)S(1)} %get-tuple-element.74), channel_id=1, source_target_pairs={{0,16},{16,32},{32,48},{48,64},{64,80},{80,96},{96,112},{112,128},... | collective-permute-start | bytes 442376 | tf_op jit(solution)/shard_map/ppermute | solution.py:524
  43.5 13.6 %all-to-all-done.in_ref = bf16[16,144,128]{2,1,0:T(8,128)(2,1)S(1)} async-done(((bf16[16,144,128]{2,1,0:T(8,128)(2,1)}), bf16[16,144,128]{2,1,0:T(8,128)(2,1)S(1)}, u32[]{:S(2)}, u32[]{:S(2)}) %all-to-all-start) | async-done | bytes 589856 | tf_op jit(solution)/shard_map/all_to_all | solution.py:526
  57.0 0.7 shard_map.266
  57.7 6.3 %all-to-all-start.1 = ((bf16[16,32,128]{2,1,0:T(8,128)(2,1)}), bf16[16,32,128]{2,1,0:T(8,128)(2,1)S(1)}, u32[]{:S(2)}, u32[]{:S(2)}) async-start(bf16[16,32,128]{2,1,0:T(8,128)(2,1)} %get-tuple-element.92), calls=%async_computation.1 | async-start | bytes 262144 | tf_op jit(solution)/shard_map/all_to_all | solution.py:533
  64.0 5.0 %collective-permute-start.10 = (bf16[112,128]{1,0:T(8,128)(2,1)S(1)}, bf16[112,128]{1,0:T(8,128)(2,1)S(1)}, u32[]{:S(2)}, u32[]{:S(2)}) collective-permute-start(bf16[112,128]{1,0:T(8,128)(2,1)S(1)} %get-tuple-element.79.refs_0_), channel_id=1, source_target_pairs={{0,13},{1,12},{4,9},{5,8},{8,5},{9,4},{12,1},{13,0},{2,15},{3,14},... | collective-permute-start | bytes 86024 | tf_op jit(solution)/shard_map/ppermute | solution.py:531
  69.0 0.5 collective-permute-start.4
  69.5 0.0 collective-permute-start.5
  69.5 3.6 %collective-permute-start.6 = (bf16[112,128]{1,0:T(8,128)(2,1)S(1)}, bf16[112,128]{1,0:T(8,128)(2,1)S(1)}, u32[]{:S(2)}, u32[]{:S(2)}) collective-permute-start(bf16[112,128]{1,0:T(8,128)(2,1)S(1)} %get-tuple-element.79.refs_0_), channel_id=1, source_target_pairs={{0,5},{1,4},{4,1},{5,0},{8,13},{9,12},{12,9},{13,8},{2,7},{3,6},{6... | collective-permute-start | bytes 86024 | tf_op jit(solution)/shard_map/ppermute | solution.py:531
  73.1 0.0 collective-permute-done.10.refs_7_
  73.1 0.3 collective-permute-start.7
  73.5 0.0 collective-permute-done.4.refs_1_
  73.5 2.8 %collective-permute-start.8 = (bf16[112,128]{1,0:T(8,128)(2,1)S(1)}, bf16[112,128]{1,0:T(8,128)(2,1)S(1)}, u32[]{:S(2)}, u32[]{:S(2)}) collective-permute-start(bf16[112,128]{1,0:T(8,128)(2,1)S(1)} %get-tuple-element.79.refs_0_), channel_id=1, source_target_pairs={{0,9},{1,8},{4,13},{5,12},{8,1},{9,0},{12,5},{13,4},{2,11},{3,10},... | collective-permute-start | bytes 86024 | tf_op jit(solution)/shard_map/ppermute | solution.py:531
  76.3 0.0 collective-permute-done.5.refs_2_
  76.3 2.0 %collective-permute-start.9 = (bf16[112,128]{1,0:T(8,128)(2,1)S(1)}, bf16[112,128]{1,0:T(8,128)(2,1)S(1)}, u32[]{:S(2)}, u32[]{:S(2)}) collective-permute-start(bf16[112,128]{1,0:T(8,128)(2,1)S(1)} %get-tuple-element.79.refs_0_), channel_id=1, source_target_pairs={{0,12},{1,13},{4,8},{5,9},{8,4},{9,5},{12,0},{13,1},{2,14},{3,15},... | collective-permute-start | bytes 86024 | tf_op jit(solution)/shard_map/ppermute | solution.py:531
  78.3 0.3 slice.25
  78.6 0.0 collective-permute-done.6.refs_3_
  78.6 0.0 collective-permute-done.7.refs_4_
  78.6 1.5 %collective-permute-done.8.refs_5_ = bf16[112,128]{1,0:T(8,128)(2,1)S(1)} collective-permute-done((bf16[112,128]{1,0:T(8,128)(2,1)S(1)}, bf16[112,128]{1,0:T(8,128)(2,1)S(1)}, u32[]{:S(2)}, u32[]{:S(2)}) %collective-permute-start.8) | collective-permute-done | bytes 28704 | tf_op jit(solution)/shard_map/ppermute | solution.py:531
  80.1 0.3 collective-permute-done.9.refs_6_
  80.4 0.1 shard_map.267.own_ref
  80.5 5.0 %collective-permute-start.11 = (bf16[112,128]{1,0:T(8,128)(2,1)S(1)}, bf16[112,128]{1,0:T(8,128)(2,1)S(1)}, u32[]{:S(2)}, u32[]{:S(2)}) collective-permute-start(bf16[112,128]{1,0:T(8,128)(2,1)S(1)} %shard_map.267.own_ref), channel_id=1, source_target_pairs={{0,2},{2,0},{1,3},{3,1},{4,6},{6,4},{5,7},{7,5},{8,10},{10,8},{9,1... | collective-permute-start | bytes 86024 | tf_op jit(solution)/shard_map/ppermute | solution.py:538
  85.5 0.0 collective-permute-done.1
  85.5 1.1 %pad_maximum_fusion = (bf16[1,4,6,24,192]{4,3,2,1,0:T(8,128)(2,1)}, bf16[1,4,6,24,192]{4,3,2,1,0:T(8,128)(2,1)}) fusion(bf16[2,4,6,18,192]{4,3,2,1,0:T(8,128)(2,1)S(1)} %slice.25, bf16[2,4,6,6,192]{4,3,2,1,0:T(8,128)(2,1)S(1)} %bitcast.26), kind=kLoop, calls=%fused_computation.3 | loop fusion | flops 884736 | bytes 884736 | tf_op jit(solution)/shard_map/concatenate | solution.py:552
  86.6 0.0 collective-permute-done.11.got_ref
  86.6 0.7 shard_map.268
  87.4 0.0 all-to-all-done.1
  87.4 1.1 %shard_map.269 = f32[1728,23]{1,0:T(8,128)} custom-call(bf16[512,128]{1,0:T(8,128)(2,1)S(1)} %bitcast.20), custom_call_target="tpu_custom_call" | custom-call | tf_op jit(solution)/shard_map/pallas_call | solution.py:464
  (1 shorter events, 0.0 us)
Async XLA Ops:
  0.6 13.0 %copy-start = (bf16[1,4,6,24,192]{4,3,2,1,0:T(8,128)(2,1)S(1)}, bf16[1,4,6,24,192]{4,3,2,1,0:T(8,128)(2,1)}, u32[]{:S(2)}) copy-start(bf16[1,4,6,24,192]{4,3,2,1,0:T(8,128)(2,1)} %param.15) | copy-start | bytes 663556
  0.7 13.0 %copy-start.1 = (bf16[1,4,6,24,192]{4,3,2,1,0:T(8,128)(2,1)S(1)}, bf16[1,4,6,24,192]{4,3,2,1,0:T(8,128)(2,1)}, u32[]{:S(2)}) copy-start(bf16[1,4,6,24,192]{4,3,2,1,0:T(8,128)(2,1)} %param.16) | copy-start | bytes 663556
  0.7 13.0 %copy-start.2 = (f32[192]{0:T(256)S(1)}, f32[192]{0:T(256)}, u32[]{:S(2)}) copy-start(f32[192]{0:T(256)} %n1g_ref.3) | copy-start | bytes 2308
  0.7 13.0 %copy-start.5 = (f32[192]{0:T(256)S(1)}, f32[192]{0:T(256)}, u32[]{:S(2)}) copy-start(f32[192]{0:T(256)} %n1o_ref.1) | copy-start | bytes 2308
  0.7 13.0 %copy-start.3 = (f32[576]{0:T(1024)S(1)}, f32[576]{0:T(1024)}, u32[]{:S(2)}) copy-start(f32[576]{0:T(1024)} %qb_ref.1) | copy-start | bytes 6916
  0.7 13.0 %copy-start.6 = (f32[192]{0:T(256)S(1)}, f32[192]{0:T(256)}, u32[]{:S(2)}) copy-start(f32[192]{0:T(256)} %pb_ref.1) | copy-start | bytes 2308
  0.7 13.0 %copy-start.7 = (f32[192]{0:T(256)S(1)}, f32[192]{0:T(256)}, u32[]{:S(2)}) copy-start(f32[192]{0:T(256)} %n2g_ref.1) | copy-start | bytes 2308
  0.7 13.0 %copy-start.8 = (f32[192]{0:T(256)S(1)}, f32[192]{0:T(256)}, u32[]{:S(2)}) copy-start(f32[192]{0:T(256)} %n2o_ref.1) | copy-start | bytes 2308
  0.7 13.0 %copy-start.4 = (f32[768]{0:T(1024)S(1)}, f32[768]{0:T(1024)}, u32[]{:S(2)}) copy-start(f32[768]{0:T(1024)} %f1b_ref.1) | copy-start | bytes 9220
  0.7 13.0 %copy-start.9 = (f32[192]{0:T(256)S(1)}, f32[192]{0:T(256)}, u32[]{:S(2)}) copy-start(f32[192]{0:T(256)} %f2b_ref.1) | copy-start | bytes 2308
  2.6 11.0 %collective-permute-start = (bf16[2,192,192]{2,1,0:T(8,128)(2,1)S(1)}, bf16[2,192,192]{2,1,0:T(8,128)(2,1)S(1)}, u32[]{:S(2)}, u32[]{:S(2)}) collective-permute-start(bf16[2,192,192]{2,1,0:T(8,128)(2,1)S(1)} %pad_maximum_fusion.1), channel_id=1, source_target_pairs={{0,240},{16,0},{32,16},{48,32},{64,48},{80,64},{96,80},{112,96},{1... | collective-permute-start | bytes 442376 | tf_op jit(solution)/shard_map/ppermute | solution.py:484
  27.3 8.1 %collective-permute-start.2 = (bf16[1792,128]{1,0:T(8,128)(2,1)S(1)}, bf16[1792,128]{1,0:T(8,128)(2,1)S(1)}, u32[]{:S(2)}, u32[]{:S(2)}) collective-permute-start(bf16[1792,128]{1,0:T(8,128)(2,1)S(1)} %get-tuple-element.77), channel_id=1, source_target_pairs={{0,2},{2,0},{1,3},{3,1},{4,6},{6,4},{5,7},{7,5},{8,10},{10,8},{9,1... | collective-permute-start | bytes 1376264 | tf_op jit(solution)/shard_map/ppermute | solution.py:523
  28.9 6.5 %collective-permute-start.3 = (bf16[512,128]{1,0:T(8,128)(2,1)S(1)}, bf16[512,128]{1,0:T(8,128)(2,1)S(1)}, u32[]{:S(2)}, u32[]{:S(2)}) collective-permute-start(bf16[512,128]{1,0:T(8,128)(2,1)S(1)} %get-tuple-element.78.tab_ref), channel_id=1, source_target_pairs={{0,1},{1,0},{2,3},{3,2},{4,5},{5,4},{6,7},{7,6},{8,9},{9,8},{10,11... | collective-permute-start | bytes 393224 | tf_op jit(solution)/shard_map/ppermute | solution.py:512
  36.4 20.6 %all-to-all-start = ((bf16[16,144,128]{2,1,0:T(8,128)(2,1)}), bf16[16,144,128]{2,1,0:T(8,128)(2,1)S(1)}, u32[]{:S(2)}, u32[]{:S(2)}) async-start(bf16[16,144,128]{2,1,0:T(8,128)(2,1)} %shard_map.265), calls=%async_computation | async-start | bytes 1179648 | tf_op jit(solution)/shard_map/all_to_all | solution.py:526
  42.1 43.5 %collective-permute-start.1 = (bf16[2,192,192]{2,1,0:T(8,128)(2,1)S(1)}, bf16[2,192,192]{2,1,0:T(8,128)(2,1)S(1)}, u32[]{:S(2)}, u32[]{:S(2)}) collective-permute-start(bf16[2,192,192]{2,1,0:T(8,128)(2,1)S(1)} %get-tuple-element.74), channel_id=1, source_target_pairs={{0,16},{16,32},{32,48},{48,64},{64,80},{80,96},{96,112},{112,128},... | collective-permute-start | bytes 442376 | tf_op jit(solution)/shard_map/ppermute | solution.py:524
  57.7 29.7 %all-to-all-start.1 = ((bf16[16,32,128]{2,1,0:T(8,128)(2,1)}), bf16[16,32,128]{2,1,0:T(8,128)(2,1)S(1)}, u32[]{:S(2)}, u32[]{:S(2)}) async-start(bf16[16,32,128]{2,1,0:T(8,128)(2,1)} %get-tuple-element.92), calls=%async_computation.1 | async-start | bytes 262144 | tf_op jit(solution)/shard_map/all_to_all | solution.py:533
  64.0 9.1 %collective-permute-start.10 = (bf16[112,128]{1,0:T(8,128)(2,1)S(1)}, bf16[112,128]{1,0:T(8,128)(2,1)S(1)}, u32[]{:S(2)}, u32[]{:S(2)}) collective-permute-start(bf16[112,128]{1,0:T(8,128)(2,1)S(1)} %get-tuple-element.79.refs_0_), channel_id=1, source_target_pairs={{0,13},{1,12},{4,9},{5,8},{8,5},{9,4},{12,1},{13,0},{2,15},{3,14},... | collective-permute-start | bytes 86024 | tf_op jit(solution)/shard_map/ppermute | solution.py:531
  69.0 4.5 %collective-permute-start.4 = (bf16[112,128]{1,0:T(8,128)(2,1)S(1)}, bf16[112,128]{1,0:T(8,128)(2,1)S(1)}, u32[]{:S(2)}, u32[]{:S(2)}) collective-permute-start(bf16[112,128]{1,0:T(8,128)(2,1)S(1)} %get-tuple-element.79.refs_0_), channel_id=1, source_target_pairs={{0,1},{1,0},{4,5},{5,4},{8,9},{9,8},{12,13},{13,12},{2,3},{3,2},{6... | collective-permute-start | bytes 86024 | tf_op jit(solution)/shard_map/ppermute | solution.py:531
  69.5 6.9 %collective-permute-start.5 = (bf16[112,128]{1,0:T(8,128)(2,1)S(1)}, bf16[112,128]{1,0:T(8,128)(2,1)S(1)}, u32[]{:S(2)}, u32[]{:S(2)}) collective-permute-start(bf16[112,128]{1,0:T(8,128)(2,1)S(1)} %get-tuple-element.79.refs_0_), channel_id=1, source_target_pairs={{0,4},{1,5},{4,0},{5,1},{8,12},{9,13},{12,8},{13,9},{2,6},{3,7},{6... | collective-permute-start | bytes 86024 | tf_op jit(solution)/shard_map/ppermute | solution.py:531
  69.5 9.1 %collective-permute-start.6 = (bf16[112,128]{1,0:T(8,128)(2,1)S(1)}, bf16[112,128]{1,0:T(8,128)(2,1)S(1)}, u32[]{:S(2)}, u32[]{:S(2)}) collective-permute-start(bf16[112,128]{1,0:T(8,128)(2,1)S(1)} %get-tuple-element.79.refs_0_), channel_id=1, source_target_pairs={{0,5},{1,4},{4,1},{5,0},{8,13},{9,12},{12,9},{13,8},{2,7},{3,6},{6... | collective-permute-start | bytes 86024 | tf_op jit(solution)/shard_map/ppermute | solution.py:531
  73.1 5.5 %collective-permute-start.7 = (bf16[112,128]{1,0:T(8,128)(2,1)S(1)}, bf16[112,128]{1,0:T(8,128)(2,1)S(1)}, u32[]{:S(2)}, u32[]{:S(2)}) collective-permute-start(bf16[112,128]{1,0:T(8,128)(2,1)S(1)} %get-tuple-element.79.refs_0_), channel_id=1, source_target_pairs={{0,8},{1,9},{4,12},{5,13},{8,0},{9,1},{12,4},{13,5},{2,10},{3,11},... | collective-permute-start | bytes 86024 | tf_op jit(solution)/shard_map/ppermute | solution.py:531
  73.5 6.6 %collective-permute-start.8 = (bf16[112,128]{1,0:T(8,128)(2,1)S(1)}, bf16[112,128]{1,0:T(8,128)(2,1)S(1)}, u32[]{:S(2)}, u32[]{:S(2)}) collective-permute-start(bf16[112,128]{1,0:T(8,128)(2,1)S(1)} %get-tuple-element.79.refs_0_), channel_id=1, source_target_pairs={{0,9},{1,8},{4,13},{5,12},{8,1},{9,0},{12,5},{13,4},{2,11},{3,10},... | collective-permute-start | bytes 86024 | tf_op jit(solution)/shard_map/ppermute | solution.py:531
  76.3 4.1 %collective-permute-start.9 = (bf16[112,128]{1,0:T(8,128)(2,1)S(1)}, bf16[112,128]{1,0:T(8,128)(2,1)S(1)}, u32[]{:S(2)}, u32[]{:S(2)}) collective-permute-start(bf16[112,128]{1,0:T(8,128)(2,1)S(1)} %get-tuple-element.79.refs_0_), channel_id=1, source_target_pairs={{0,12},{1,13},{4,8},{5,9},{8,4},{9,5},{12,0},{13,1},{2,14},{3,15},... | collective-permute-start | bytes 86024 | tf_op jit(solution)/shard_map/ppermute | solution.py:531
  80.5 6.2 %collective-permute-start.11 = (bf16[112,128]{1,0:T(8,128)(2,1)S(1)}, bf16[112,128]{1,0:T(8,128)(2,1)S(1)}, u32[]{:S(2)}, u32[]{:S(2)}) collective-permute-start(bf16[112,128]{1,0:T(8,128)(2,1)S(1)} %shard_map.267.own_ref), channel_id=1, source_target_pairs={{0,2},{2,0},{1,3},{3,1},{4,6},{6,4},{5,7},{7,5},{8,10},{10,8},{9,1... | collective-permute-start | bytes 86024 | tf_op jit(solution)/shard_map/ppermute | solution.py:538

commit v2 on v1

--- a/solution.py
+++ b/solution.py
@@ -52,7 +52,7 @@
 
 def prep_kernel(qkv_hbm, proj_hbm, fc1_hbm, fc2_hbm, tab_hbm,
                 wt_ref, projb_ref, fc1b_ref, fc2b_ref, bias_ref, spread_ref, mask_ref, sel_ref,
-                ra_ref, ca_ref, rb_ref, cb_ref,
+                ra_ref, ca_ref, rb_ref, cb_ref, picks_ref, back_ref,
                 qkv_ref, proj_ref, fc1_ref, fc2_ref, tab_ref, sems):
     copies = [
         pltpu.make_async_copy(src, dst, sems.at[k])
@@ -101,6 +101,8 @@
     n = iota((16, 1152), 1)
     n = whole(n - 192.0 * whole(n, 192), 12)
     rb_ref[...] = one_hot(n == iota((16, 1152), 0))
+    picks_ref[...] = window_picks()
+    back_ref[...] = natural_picks()
     copies[0].wait()
     tiles = []
     for t in range(3):
@@ -187,14 +189,14 @@
 
 def front_kernel(x_ref, cot_ref, n1g_ref, n1o_ref, qb_ref, pb_ref, n2g_ref, n2o_ref,
                  f1b_ref, f2b_ref, halo_ref, bias_ref, wt_ref, proj_ref, fc1_ref, fc2_ref,
-                 spread_ref, mask_ref, sel_ref,
+                 spread_ref, mask_ref, sel_ref, picks_ref,
                  low_ref, block_ref, few_ref, wide_ref, hat_ref, inv_ref, rg_ref, row_ref, f1s_ref,
                  sum_ref, tab_ref):
     n1g, n1o, qb, pb, n2g, n2o, f1b, f2b = (
         ref[...].reshape(1, -1)
         for ref in (n1g_ref, n1o_ref, qb_ref, pb_ref, n2g_ref, n2o_ref, f1b_ref, f2b_ref)
     )
-    picks = window_picks()
+    picks = picks_ref[...]
     xw = nn(picks, jnp.concatenate([x_ref[...], halo_ref[0]], axis=0))
     cw = nn(picks, jnp.concatenate([cot_ref[...], halo_ref[1]], axis=0))
     cot_low = cw.astype(BF16)
@@ -241,10 +243,10 @@
         rows = slice(ROWS * g, ROWS * g + ROWS)
         u = nn(normed2[rows], fc1_ref[...]) + f1b
         square = u * u
-        t = jnp.tanh(GELU_C * (u + GELU_A * (square * u)))
-        half = 0.5 * (1.0 + t)
+        half = 0.5 * jnp.tanh(u * (GELU_C + (GELU_A * GELU_C) * square)) + 0.5
         acts.append((u * half).astype(BF16))
-        slope = half + 0.5 * u * (1.0 - t * t) * (GELU_C + (3.0 * GELU_A * GELU_C) * square)
+        lean = u * (2.0 * GELU_C + (6.0 * GELU_A * GELU_C) * square)
+        slope = half + (half - half * half) * lean
         act_grad = nn(cot_low[rows], fc2_ref[...])
         pre = (act_grad * slope).astype(BF16)
         grads.append(pre)
@@ -314,9 +316,9 @@
     f1s_ref[...] = f1_sum
 
 
-def back_kernel(core_ref, n1g_ref, block_ref, few_ref, wide_ref, hat_ref, inv_ref, rg_ref, row_ref,
+def back_kernel(core_ref, n1g_ref, few_ref, wide_ref, hat_ref, inv_ref, rg_ref, row_ref,
                 f1s_ref, wt_ref, ra_ref, ca_ref, rb_ref, cb_ref,
-                out_ref, edge_ref, own_ref, send_ref, stage_ref):
+                ig_ref, own_ref, send_ref, stage_ref):
     wq = wt_ref[0:192, :]
     wk = wt_ref[192:384, :]
     wv = wt_ref[384:576, :]
@@ -331,17 +333,11 @@
     f2_sum = row_ref[1:2, :]
     n2g_sum = row_ref[2:3, :]
     n2o_sum = row_ref[3:4, :]
-    back = natural_picks()
-    placed = nn(back, block_ref[...]).astype(BF16)
-    out_ref[0] = placed[:576]
-    edge_ref[0] = placed[576:]
     n1_grad = nn(dq, wq) + nn(dk, wk) + nn(dv, wv)
     n1g_sum = jnp.sum(n1_grad * hat1, axis=0, keepdims=True)
     n1o_sum = jnp.sum(n1_grad, axis=0, keepdims=True)
     input_grad = (rg_ref[...] + norm_back(n1_grad, hat1, inv_ref[...], n1g)).astype(BF16)
-    placed = nn(back, input_grad).astype(BF16)
-    out_ref[1] = placed[:576]
-    edge_ref[1] = placed[576:]
+    ig_ref[...] = input_grad
     sums = [jnp.sum(d.astype(F32), axis=0, keepdims=True) for d in (dq, dk, dv)]
     dw_q = tn(dq, normed)
     dw_k = tn(dk, normed)
@@ -377,6 +373,25 @@
     send_ref[...] = stage_ref[1 - core].astype(BF16)
 
 
+def place_kernel(block_ref, ig_ref, back_ref, out_ref, edge_ref):
+    back = back_ref[...]
+    for k, ref in enumerate((block_ref, ig_ref)):
+        placed = nn(back, ref[...]).astype(BF16)
+        out_ref[k] = placed[:576]
+        edge_ref[k] = placed[576:]
+
+
+def edge_kernel(x_hbm, cot_hbm, out_ref, sems):
+    copies = [
+        pltpu.make_async_copy(src.at[:, 0:8, :], out_ref.at[k], sems.at[k])
+        for k, src in enumerate((x_hbm, cot_hbm))
+    ]
+    for copy in copies:
+        copy.start()
+    for copy in copies:
+        copy.wait()
+
+
 def join_kernel(own_ref, got_ref, tab_ref, twin_ref, out_ref):
     for l in range(16):
         part = slice(PART * l, PART * l + PART)
@@ -390,19 +405,16 @@
     for l in range(1, 16):
         total = total + in_ref[l].astype(F32)
     low = total.astype(BF16)
-    part_ref[...] = low[:PART]
+    for k in range(8):
+        part_ref[k] = low[:PART]
     for k in range(16):
         tab_ref[k] = low[PART:]
 
 
-def band_sum_kernel(slot_ref, *refs):
-    out_ref, all_ref = refs[8], refs[9]
-    slot = slot_ref[0]
-    for k in range(8):
-        all_ref[jnp.bitwise_xor(slot, k)] = refs[k][...].astype(F32)
-    total = all_ref[0]
+def band_sum_kernel(in_ref, out_ref):
+    total = in_ref[0].astype(F32)
     for k in range(1, 8):
-        total = total + all_ref[k]
+        total = total + in_ref[k].astype(F32)
     out_ref[...] = total.astype(BF16)
 
 
@@ -480,15 +492,18 @@
     grid = inputs.shape
     x = inputs.reshape(576, C)
     cot = cotangent.reshape(576, C)
-    edge = jnp.stack([inputs[0, :, :, :8, :].reshape(192, C), cotangent[0, :, :, :8, :].reshape(192, C)])
+    edge = call(
+        edge_kernel, near((2, 24, 8, C), BF16), far=2, raw=True,
+        scratch=[pltpu.SemaphoreType.DMA((2,))],
+    )(inputs.reshape(24, 24, C), cotangent.reshape(24, 24, C)).reshape(2, 192, C)
     halo = lax.ppermute(edge, "lon", [(k, (k - 1) % 16) for k in range(16)])
     table = bias_table.reshape(12 * ROWS, 23)
-    wt, proj, fc1, fc2, bias, spread, mask, sel, ra, ca, rb, cb = call(
+    wt, proj, fc1, fc2, bias, spread, mask, sel, ra, ca, rb, cb, picks, back = call(
         prep_kernel,
         [near((576, C), BF16), near((C, C), BF16), near((C, FF), BF16), near((C, FF), BF16),
          near((2, ROWS, LANES), F32), near((ROWS, LANES), BF16), near((C, LANES), BF16),
          near((12 * ROWS, TAB), BF16), near((16, 1344), BF16), near((1344, 128), BF16),
-         near((16, 1152), BF16), near((1152, 128), BF16)],
+         near((16, 1152), BF16), near((1152, 128), BF16), near((576, 768), BF16), near((768, 576), BF16)],
         far=5,
         limit=16,
         raw=True,
@@ -497,44 +512,40 @@
                  pltpu.SemaphoreType.DMA((5,))],
     )(qkv_weight, proj_weight, fc1_weight, fc2_weight.T, table)
     core = lax.axis_index("core").astype(jnp.int32).reshape(1)
-    slot = (2 * lax.axis_index("y") + lax.axis_index("ens")).astype(jnp.int32).reshape(1)
-    tab, *state = call(
+    tab, block, *state = call(
         front_kernel,
         [near((16 * SLOT, 128), BF16), near((576, C), BF16), near((8, 576, C), BF16),
          near((2, 576, FF), BF16), near((576, C), F32), near((576, 1), F32), near((576, C), F32),
          near((8, C), F32), near((1, FF), F32)],
         far=10,
-        near=9,
+        near=10,
         limit=24,
         scratch=[pltpu.VMEM((2, ROWS, LANES), F32), pltpu.VMEM((16 * SLOT, 128), F32)],
     )(x, cot, norm1_gain, norm1_offset, qkv_bias, proj_bias, norm2_gain, norm2_offset, fc1_bias,
-      fc2_bias, halo, bias, wt, proj, fc1, fc2, spread, mask, sel)
+      fc2_bias, halo, bias, wt, proj, fc1, fc2, spread, mask, sel, picks)
     twin = lax.ppermute(tab, "ens", [(0, 1), (1, 0)])
-    both, ends, own, send = call(
+    slope, own, send = call(
         back_kernel,
-        [shape((2, 576, C), BF16), near((2, 192, C), BF16), near((16 * PART, 128), BF16),
-         near((16 * PART, 128), BF16)],
+        [near((576, C), BF16), near((16 * PART, 128), BF16), near((16 * PART, 128), BF16)],
         smem=1,
         far=1,
-        near=13,
+        near=12,
         limit=16,
         scratch=[pltpu.VMEM((2, 16 * PART, 128), F32)],
     )(core, norm1_gain, *state, wt, ra, ca, rb, cb)
     got = lax.ppermute(send, "core", [(0, 1), (1, 0)])
-    home = lax.ppermute(ends, "lon", [(k, (k + 1) % 16) for k in range(16)])
     joined = call(join_kernel, near((16, PART + SLOT, 128), BF16), near=4)(own, got, tab, twin)
     arrived = lax.all_to_all(joined, "lon", split_axis=0, concat_axis=0, tiled=True)
+    both, ends = call(
+        place_kernel, [near((2, 576, C), BF16), near((2, 192, C), BF16)], near=3
+    )(block, slope, back)
+    home = lax.ppermute(ends, "lon", [(k, (k + 1) % 16) for k in range(16)])
     part, tab_copies = call(
-        lon_sum_kernel, [near((PART, 128), BF16), near((16, SLOT, 128), BF16)], near=1
+        lon_sum_kernel, [near((8, PART, 128), BF16), near((16, SLOT, 128), BF16)], near=1
     )(arrived)
-    bands = [part] + [
-        lax.ppermute(part, ("y", "ens"), [(n, n ^ k) for n in range(8)]) for k in range(1, 8)
-    ]
+    bands = lax.all_to_all(part, ("y", "ens"), split_axis=0, concat_axis=0, tiled=True)
     tab_all = lax.all_to_all(tab_copies, "lon", split_axis=0, concat_axis=0, tiled=True)
-    half = call(
-        band_sum_kernel, near((PART, 128), BF16), smem=1, near=8,
-        scratch=[pltpu.VMEM((8, PART, 128), F32)],
-    )(slot, *bands)
+    half = call(band_sum_kernel, near((PART, 128), BF16), near=1)(bands)
     other = lax.ppermute(half, "core", [(0, 1), (1, 0)])
     qw, pw, f1, f2, qb, pb, f1b, f2b, n1g, n1o, n2g, n2o = call(
         weight_kernel,

time: 88.8 us -> 87.9 us (0.990)
  the two profiles are of different devices: /device:TPU:1 before, /device:TPU:2 now
where the time goes in v2:
time: 87.9 us; the launch traced here: 87.6 us
  blocking collectives  24.9 us (28%)
  Pallas kernels  20.4 us (23%)
  starting transfers between devices  20.4 us (23%)
  waiting for transfers between devices  19.6 us (22%)
  other arithmetic  1.1 us (1%)
    all_to_all x1, blocking collectives, on_device(): lax.all_to_all(joined, 'lon', split_axis=0, concat_axis=0, tiled=True)  24.9 us
    pallas_call x10, Pallas kernels, go(): return run(*kept)  20.4 us
    all_to_all x1, waiting for transfers between devices, on_device(): lax.all_to_all(part, ('y', 'ens'), split_axis=0, concat_axis=0, tiled=True)  8.62 us
    all_to_all x1, starting transfers between devices, on_device(): lax.all_to_all(part, ('y', 'ens'), split_axis=0, concat_axis=0, tiled=True)  6.03 us
    ppermute x1, starting transfers between devices, on_device(): halo = lax.ppermute(edge, 'lon', [(k, (k - 1) % 16) for k in range(16)])  5.9 us
    all_to_all x1, waiting for transfers between devices, on_device(): lax.all_to_all(tab_copies, 'lon', split_axis=0, concat_axis=0, tiled=True)  5.25 us
    all_to_all x1, starting transfers between devices, on_device(): lax.all_to_all(tab_copies, 'lon', split_axis=0, concat_axis=0, tiled=True)  4.93 us
    ppermute x1, waiting for transfers between devices, on_device(): twin = lax.ppermute(tab, 'ens', [(0, 1), (1, 0)])  4.88 us
  transfers between devices with their start and end apart: 7, of which 5 were waited for; matrix products, arithmetic and copies ran while one was open for 2% of the time, Pallas kernels for 6%

profile of v2, /device:TPU:2, one launch (start us, length us, event | category | flops | bytes accessed | tf_op | source)
XLA Modules:
  0.0 87.6 jit_solution(3060325698275437082)
XLA Ops:
  0.6 0.0 copy-start
  0.7 0.0 copy-start.1
  0.7 0.0 copy-start.2
  0.7 0.0 copy-start.3
  0.7 0.0 copy-start.4
  0.7 0.0 copy-start.5
  0.7 0.0 copy-start.6
  0.7 0.0 copy-start.7
  0.7 0.0 copy-start.8
  0.7 0.0 copy-start.9
  0.7 1.0 %shard_map.262 = bf16[2,24,8,192]{3,2,1,0:T(8,128)(2,1)S(1)} custom-call(bf16[24,24,192]{2,1,0:T(8,128)(2,1)} %bitcast.17, bf16[24,24,192]{2,1,0:T(8,128)(2,1)} %bitcast.19), custom_call_target="tpu_custom_call" | custom-call | tf_op jit(solution)/shard_map/pallas_call | solution.py:476
  1.8 5.9 %collective-permute-start = (bf16[2,192,192]{2,1,0:T(8,128)(2,1)S(1)}, bf16[2,192,192]{2,1,0:T(8,128)(2,1)S(1)}, u32[]{:S(2)}, u32[]{:S(2)}) collective-permute-start(bf16[2,192,192]{2,1,0:T(8,128)(2,1)S(1)} %bitcast.23), channel_id=1, source_target_pairs={{0,240},{16,0},{32,16},{48,32},{64,48},{80,64},{96,80},{112,96},{1... | collective-permute-start | bytes 442376 | tf_op jit(solution)/shard_map/ppermute | solution.py:499
  7.7 3.4 %shard_map.263 = (bf16[576,192]{1,0:T(8,128)(2,1)S(1)}, bf16[192,192]{1,0:T(8,128)(2,1)S(1)}, bf16[192,768]{1,0:T(8,128)(2,1)S(1)}, bf16[192,768]{1,0:T(8,128)(2...) custom-call(f32[192,576]{1,0:T(8,128)} %qkv_hbm.1, ...), custom_call_target="tpu_custom_call" | custom-call | tf_op jit(solution)/shard_map/pallas_call | solution.py:476
  11.1 0.7 collective-permute-done.halo_ref
  11.8 0.0 copy-done
  11.8 0.0 copy-done.1
  11.8 0.0 copy-done.2
  11.8 0.0 copy-done.3
  11.8 0.0 copy-done.4
  11.9 0.0 copy-done.5
  11.9 0.0 copy-done.6
  11.9 0.0 copy-done.7
  11.9 0.0 copy-done.8
  11.9 0.0 copy-done.9
  11.9 10.8 %shard_map.264 = (bf16[512,128]{1,0:T(8,128)(2,1)S(1)}, bf16[576,192]{1,0:T(8,128)(2,1)S(1)}, bf16[8,576,192]{2,1,0:T(8,128)(2,1)S(1)}, bf16[2,576,768]{2,1,0:T(...) custom-call(bf16[576,192]{1,0:T(8,128)(2,1)S(1)} %bitcast.18, ...), custom_call_target="tpu_custom_call" | custom-call | tf_op jit(solution)/shard_map/pallas_call | solution.py:476
  22.7 1.6 %shard_map.265 = (bf16[576,192]{1,0:T(8,128)(2,1)S(1)}, bf16[1792,128]{1,0:T(8,128)(2,1)S(1)}, bf16[1792,128]{1,0:T(8,128)(2,1)S(1)}) custom-call(s32[1]{0:T(128)} %bitcast.7.core_ref, f32[192]{0:T(256)S(1)} %copy-done.4, bf16[8,576,192]{2,1,0:T(8,128)(2,1)S(1)} %get-tuple-element.67.few_ref, bf16[2,576,768]{2,1,0:T(8,128)(2,1)S(1)} %get-tuple-element.68.wide_ref, ...), custom_call_target="tpu_custom_call" | custom-call | tf_op jit(solution)/shard_map/pallas_call | solution.py:476
  24.3 0.1 collective-permute-start.2
  24.4 2.5 %collective-permute-start.3 = (bf16[512,128]{1,0:T(8,128)(2,1)S(1)}, bf16[512,128]{1,0:T(8,128)(2,1)S(1)}, u32[]{:S(2)}, u32[]{:S(2)}) collective-permute-start(bf16[512,128]{1,0:T(8,128)(2,1)S(1)} %get-tuple-element.84.tab_ref), channel_id=1, source_target_pairs={{0,1},{1,0},{2,3},{3,2},{4,5},{5,4},{6,7},{7,6},{8,9},{9,8},{10,11... | collective-permute-start | bytes 393224 | tf_op jit(solution)/shard_map/ppermute | solution.py:526
  26.9 4.9 %collective-permute-done.3.twin_ref = bf16[512,128]{1,0:T(8,128)(2,1)S(1)} collective-permute-done((bf16[512,128]{1,0:T(8,128)(2,1)S(1)}, bf16[512,128]{1,0:T(8,128)(2,1)S(1)}, u32[]{:S(2)}, u32[]{:S(2)}) %collective-permute-start.3) | collective-permute-done | bytes 131104 | tf_op jit(solution)/shard_map/ppermute | solution.py:526
  31.8 0.0 collective-permute-done.2.got_ref
  31.8 0.1 shard_map.267
  31.9 24.9 %all_to_all.15.in_ref = bf16[16,144,128]{2,1,0:T(8,128)(2,1)S(1)} all-to-all(bf16[16,144,128]{2,1,0:T(8,128)(2,1)S(1)} %shard_map.267), channel_id=1, replica_groups=mesh['lon'=16,'y'=4,'core'=2,'ens'=2] {'lon'}, dimensions={0} | all-to-all | bytes 1179648 | tf_op jit(solution)/shard_map/all_to_all | solution.py:538
  56.9 0.8 shard_map.268
  57.7 6.0 %all-to-all-start.1 = ((bf16[8,112,128]{2,1,0:T(8,128)(2,1)}), bf16[8,112,128]{2,1,0:T(8,128)(2,1)S(1)}, u32[]{:S(2)}, u32[]{:S(2)}) async-start(bf16[8,112,128]{2,1,0:T(8,128)(2,1)} %get-tuple-element.85), calls=%async_computation.1 | async-start | bytes 458752 | tf_op jit(solution)/shard_map/all_to_all | solution.py:546
  63.7 0.8 shard_map.266
  64.5 0.9 collective-permute-start.1
  65.4 8.6 %all-to-all-done.1.in_ref = bf16[8,112,128]{2,1,0:T(8,128)(2,1)S(1)} async-done(((bf16[8,112,128]{2,1,0:T(8,128)(2,1)}), bf16[8,112,128]{2,1,0:T(8,128)(2,1)S(1)}, u32[]{:S(2)}, u32[]{:S(2)}) %all-to-all-start.1) | async-done | bytes 229408 | tf_op jit(solution)/shard_map/all_to_all | solution.py:546
  74.0 4.9 %all-to-all-start.2 = ((bf16[16,32,128]{2,1,0:T(8,128)(2,1)}), bf16[16,32,128]{2,1,0:T(8,128)(2,1)S(1)}, u32[]{:S(2)}, u32[]{:S(2)}) async-start(bf16[16,32,128]{2,1,0:T(8,128)(2,1)} %get-tuple-element.98), calls=%async_computation.2 | async-start | bytes 262144 | tf_op jit(solution)/shard_map/all_to_all | solution.py:547
  78.9 0.3 slice.17
  79.2 0.1 collective-permute-start.4
  79.3 0.0 collective-permute-done.1
  79.3 1.1 %pad_maximum_fusion = (bf16[1,4,6,24,192]{4,3,2,1,0:T(8,128)(2,1)}, bf16[1,4,6,24,192]{4,3,2,1,0:T(8,128)(2,1)}) fusion(bf16[2,4,6,18,192]{4,3,2,1,0:T(8,128)(2,1)S(1)} %slice.17, bf16[2,4,6,6,192]{4,3,2,1,0:T(8,128)(2,1)S(1)} %bitcast.27), kind=kLoop, calls=%fused_computation.3 | loop fusion | flops 884736 | bytes 884736 | tf_op jit(solution)/shard_map/concatenate | solution.py:563
  80.4 0.1 collective-permute-done.4.got_ref
  80.5 0.7 shard_map.270
  81.2 5.3 %all-to-all-done.2 = bf16[16,32,128]{2,1,0:T(8,128)(2,1)S(1)} async-done(((bf16[16,32,128]{2,1,0:T(8,128)(2,1)}), bf16[16,32,128]{2,1,0:T(8,128)(2,1)S(1)}, u32[]{:S(2)}, u32[]{:S(2)}) %all-to-all-start.2) | async-done | bytes 131104 | tf_op jit(solution)/shard_map/all_to_all | solution.py:547
  86.5 1.1 %shard_map.271 = f32[1728,23]{1,0:T(8,128)} custom-call(bf16[512,128]{1,0:T(8,128)(2,1)S(1)} %bitcast.22), custom_call_target="tpu_custom_call" | custom-call | tf_op jit(solution)/shard_map/pallas_call | solution.py:476
  (1 shorter events, 0.0 us)
Async XLA Ops:
  0.6 11.2 %copy-start = (bf16[1,4,6,24,192]{4,3,2,1,0:T(8,128)(2,1)S(1)}, bf16[1,4,6,24,192]{4,3,2,1,0:T(8,128)(2,1)}, u32[]{:S(2)}) copy-start(bf16[1,4,6,24,192]{4,3,2,1,0:T(8,128)(2,1)} %param.15) | copy-start | bytes 663556
  0.7 11.2 %copy-start.1 = (bf16[1,4,6,24,192]{4,3,2,1,0:T(8,128)(2,1)S(1)}, bf16[1,4,6,24,192]{4,3,2,1,0:T(8,128)(2,1)}, u32[]{:S(2)}) copy-start(bf16[1,4,6,24,192]{4,3,2,1,0:T(8,128)(2,1)} %param.16) | copy-start | bytes 663556
  0.7 11.2 %copy-start.2 = (f32[576]{0:T(1024)S(1)}, f32[576]{0:T(1024)}, u32[]{:S(2)}) copy-start(f32[576]{0:T(1024)} %qb_ref.1) | copy-start | bytes 6916
  0.7 11.2 %copy-start.3 = (f32[768]{0:T(1024)S(1)}, f32[768]{0:T(1024)}, u32[]{:S(2)}) copy-start(f32[768]{0:T(1024)} %f1b_ref.1) | copy-start | bytes 9220
  0.7 11.2 %copy-start.4 = (f32[192]{0:T(256)S(1)}, f32[192]{0:T(256)}, u32[]{:S(2)}) copy-start(f32[192]{0:T(256)} %n1g_ref.3) | copy-start | bytes 2308
  0.7 11.2 %copy-start.5 = (f32[192]{0:T(256)S(1)}, f32[192]{0:T(256)}, u32[]{:S(2)}) copy-start(f32[192]{0:T(256)} %n1o_ref.1) | copy-start | bytes 2308
  0.7 11.2 %copy-start.6 = (f32[192]{0:T(256)S(1)}, f32[192]{0:T(256)}, u32[]{:S(2)}) copy-start(f32[192]{0:T(256)} %pb_ref.1) | copy-start | bytes 2308
  0.7 11.2 %copy-start.7 = (f32[192]{0:T(256)S(1)}, f32[192]{0:T(256)}, u32[]{:S(2)}) copy-start(f32[192]{0:T(256)} %n2g_ref.1) | copy-start | bytes 2308
  0.7 11.2 %copy-start.8 = (f32[192]{0:T(256)S(1)}, f32[192]{0:T(256)}, u32[]{:S(2)}) copy-start(f32[192]{0:T(256)} %n2o_ref.1) | copy-start | bytes 2308
  0.7 11.2 %copy-start.9 = (f32[192]{0:T(256)S(1)}, f32[192]{0:T(256)}, u32[]{:S(2)}) copy-start(f32[192]{0:T(256)} %f2b_ref.1) | copy-start | bytes 2308
  1.8 10.1 %collective-permute-start = (bf16[2,192,192]{2,1,0:T(8,128)(2,1)S(1)}, bf16[2,192,192]{2,1,0:T(8,128)(2,1)S(1)}, u32[]{:S(2)}, u32[]{:S(2)}) collective-permute-start(bf16[2,192,192]{2,1,0:T(8,128)(2,1)S(1)} %bitcast.23), channel_id=1, source_target_pairs={{0,240},{16,0},{32,16},{48,32},{64,48},{80,64},{96,80},{112,96},{1... | collective-permute-start | bytes 442376 | tf_op jit(solution)/shard_map/ppermute | solution.py:499
  24.3 7.5 %collective-permute-start.2 = (bf16[1792,128]{1,0:T(8,128)(2,1)S(1)}, bf16[1792,128]{1,0:T(8,128)(2,1)S(1)}, u32[]{:S(2)}, u32[]{:S(2)}) collective-permute-start(bf16[1792,128]{1,0:T(8,128)(2,1)S(1)} %get-tuple-element.83), channel_id=1, source_target_pairs={{0,2},{2,0},{1,3},{3,1},{4,6},{6,4},{5,7},{7,5},{8,10},{10,8},{9,1... | collective-permute-start | bytes 1376264 | tf_op jit(solution)/shard_map/ppermute | solution.py:536
  24.4 7.4 %collective-permute-start.3 = (bf16[512,128]{1,0:T(8,128)(2,1)S(1)}, bf16[512,128]{1,0:T(8,128)(2,1)S(1)}, u32[]{:S(2)}, u32[]{:S(2)}) collective-permute-start(bf16[512,128]{1,0:T(8,128)(2,1)S(1)} %get-tuple-element.84.tab_ref), channel_id=1, source_target_pairs={{0,1},{1,0},{2,3},{3,2},{4,5},{5,4},{6,7},{7,6},{8,9},{9,8},{10,11... | collective-permute-start | bytes 393224 | tf_op jit(solution)/shard_map/ppermute | solution.py:526
  57.7 16.3 %all-to-all-start.1 = ((bf16[8,112,128]{2,1,0:T(8,128)(2,1)}), bf16[8,112,128]{2,1,0:T(8,128)(2,1)S(1)}, u32[]{:S(2)}, u32[]{:S(2)}) async-start(bf16[8,112,128]{2,1,0:T(8,128)(2,1)} %get-tuple-element.85), calls=%async_computation.1 | async-start | bytes 458752 | tf_op jit(solution)/shard_map/all_to_all | solution.py:546
  64.5 14.8 %collective-permute-start.1 = (bf16[2,192,192]{2,1,0:T(8,128)(2,1)S(1)}, bf16[2,192,192]{2,1,0:T(8,128)(2,1)S(1)}, u32[]{:S(2)}, u32[]{:S(2)}) collective-permute-start(bf16[2,192,192]{2,1,0:T(8,128)(2,1)S(1)} %get-tuple-element.80), channel_id=1, source_target_pairs={{0,16},{16,32},{32,48},{48,64},{64,80},{80,96},{96,112},{112,128},... | collective-permute-start | bytes 442376 | tf_op jit(solution)/shard_map/ppermute | solution.py:542
  74.0 12.5 %all-to-all-start.2 = ((bf16[16,32,128]{2,1,0:T(8,128)(2,1)}), bf16[16,32,128]{2,1,0:T(8,128)(2,1)S(1)}, u32[]{:S(2)}, u32[]{:S(2)}) async-start(bf16[16,32,128]{2,1,0:T(8,128)(2,1)} %get-tuple-element.98), calls=%async_computation.2 | async-start | bytes 262144 | tf_op jit(solution)/shard_map/all_to_all | solution.py:547
  79.2 1.3 %collective-permute-start.4 = (bf16[112,128]{1,0:T(8,128)(2,1)S(1)}, bf16[112,128]{1,0:T(8,128)(2,1)S(1)}, u32[]{:S(2)}, u32[]{:S(2)}) collective-permute-start(bf16[112,128]{1,0:T(8,128)(2,1)S(1)} %shard_map.269.own_ref), channel_id=1, source_target_pairs={{0,2},{2,0},{1,3},{3,1},{4,6},{6,4},{5,7},{7,5},{8,10},{10,8},{9,1... | collective-permute-start | bytes 86024 | tf_op jit(solution)/shard_map/ppermute | solution.py:549

commit v3 on v2

--- a/solution.py
+++ b/solution.py
@@ -295,7 +295,8 @@
         for t in range(3):
             tab_ref[ROWS * t + HX * v : ROWS * t + HX * v + HX, :] = total[:, 128 * t : 128 * t + 128]
     tab_ref[3 * ROWS :, :] = jnp.zeros((16 * SLOT - 3 * ROWS, 128), F32)
-    low_ref[...] = tab_ref[...].astype(BF16)
+    for l in range(16):
+        low_ref[l] = tab_ref[SLOT * l : SLOT * l + SLOT, :].astype(BF16)
     for k, group in enumerate((grad_q, grad_k, grad_v)):
         for g in range(4):
             few_ref[k, ROWS * g : ROWS * g + ROWS, :] = group[g]
@@ -317,8 +318,9 @@
 
 
 def back_kernel(core_ref, n1g_ref, few_ref, wide_ref, hat_ref, inv_ref, rg_ref, row_ref,
-                f1s_ref, wt_ref, ra_ref, ca_ref, rb_ref, cb_ref,
-                ig_ref, own_ref, send_ref, stage_ref):
+                f1s_ref, wt_ref, ra_ref, ca_ref, rb_ref, cb_ref, low_ref,
+                ig_ref, own_ref, send_ref, tab_ref, stage_ref):
+    tab_ref[...] = low_ref[...]
     wq = wt_ref[0:192, :]
     wk = wt_ref[192:384, :]
     wv = wt_ref[384:576, :]
@@ -392,23 +394,26 @@
         copy.wait()
 
 
-def join_kernel(own_ref, got_ref, tab_ref, twin_ref, out_ref):
+def join_kernel(own_ref, got_ref, tab_ref, out_ref):
+    table = tab_ref[0].astype(F32)
+    for l in range(1, 16):
+        table = table + tab_ref[l].astype(F32)
+    low = table.astype(BF16)
     for l in range(16):
         part = slice(PART * l, PART * l + PART)
         out_ref[l, 0:PART, :] = (own_ref[part].astype(F32) + got_ref[part].astype(F32)).astype(BF16)
-        spot = slice(SLOT * l, SLOT * l + SLOT)
-        out_ref[l, PART:, :] = (tab_ref[spot].astype(F32) + twin_ref[spot].astype(F32)).astype(BF16)
+        out_ref[l, PART:, :] = low
 
 
 def lon_sum_kernel(in_ref, part_ref, tab_ref):
-    total = in_ref[0].astype(F32)
+    total = in_ref[0, 0:PART].astype(F32)
     for l in range(1, 16):
-        total = total + in_ref[l].astype(F32)
+        total = total + in_ref[l, 0:PART].astype(F32)
     low = total.astype(BF16)
     for k in range(8):
-        part_ref[k] = low[:PART]
-    for k in range(16):
-        tab_ref[k] = low[PART:]
+        part_ref[k] = low
+    for l in range(16):
+        tab_ref[SLOT * l : SLOT * l + SLOT, :] = in_ref[l, PART:]
 
 
 def band_sum_kernel(in_ref, out_ref):
@@ -439,8 +444,8 @@
         ref[...] = vb[:, 12 * k : 12 * k + 12].reshape(12)
 
 
-def table_kernel(tab_ref, out_tab_ref):
-    tab = tab_ref[...].astype(F32)
+def table_kernel(tab_ref, twin_ref, out_tab_ref):
+    tab = tab_ref[...].astype(F32) + twin_ref[...].astype(F32)
     for t in range(3):
         tile = tab[ROWS * t : ROWS * t + ROWS]
         for k in range(4):
@@ -514,7 +519,7 @@
     core = lax.axis_index("core").astype(jnp.int32).reshape(1)
     tab, block, *state = call(
         front_kernel,
-        [near((16 * SLOT, 128), BF16), near((576, C), BF16), near((8, 576, C), BF16),
+        [near((16, SLOT, 128), BF16), near((576, C), BF16), near((8, 576, C), BF16),
          near((2, 576, FF), BF16), near((576, C), F32), near((576, 1), F32), near((576, C), F32),
          near((8, C), F32), near((1, FF), F32)],
         far=10,
@@ -523,28 +528,29 @@
         scratch=[pltpu.VMEM((2, ROWS, LANES), F32), pltpu.VMEM((16 * SLOT, 128), F32)],
     )(x, cot, norm1_gain, norm1_offset, qkv_bias, proj_bias, norm2_gain, norm2_offset, fc1_bias,
       fc2_bias, halo, bias, wt, proj, fc1, fc2, spread, mask, sel, picks)
-    twin = lax.ppermute(tab, "ens", [(0, 1), (1, 0)])
-    slope, own, send = call(
+    slope, own, send, tab = call(
         back_kernel,
-        [near((576, C), BF16), near((16 * PART, 128), BF16), near((16 * PART, 128), BF16)],
+        [near((576, C), BF16), near((16 * PART, 128), BF16), near((16 * PART, 128), BF16),
+         shape((16, SLOT, 128), BF16)],
         smem=1,
         far=1,
-        near=12,
+        near=13,
         limit=16,
         scratch=[pltpu.VMEM((2, 16 * PART, 128), F32)],
-    )(core, norm1_gain, *state, wt, ra, ca, rb, cb)
+    )(core, norm1_gain, *state, wt, ra, ca, rb, cb, tab)
+    tab = lax.all_to_all(tab, "lon", split_axis=0, concat_axis=0, tiled=True)
     got = lax.ppermute(send, "core", [(0, 1), (1, 0)])
-    joined = call(join_kernel, near((16, PART + SLOT, 128), BF16), near=4)(own, got, tab, twin)
+    joined = call(join_kernel, near((16, PART + SLOT, 128), BF16), near=3)(own, got, tab)
     arrived = lax.all_to_all(joined, "lon", split_axis=0, concat_axis=0, tiled=True)
     both, ends = call(
         place_kernel, [near((2, 576, C), BF16), near((2, 192, C), BF16)], near=3
     )(block, slope, back)
     home = lax.ppermute(ends, "lon", [(k, (k + 1) % 16) for k in range(16)])
-    part, tab_copies = call(
-        lon_sum_kernel, [near((8, PART, 128), BF16), near((16, SLOT, 128), BF16)], near=1
+    part, tab_all = call(
+        lon_sum_kernel, [near((8, PART, 128), BF16), near((16 * SLOT, 128), BF16)], near=1
     )(arrived)
     bands = lax.all_to_all(part, ("y", "ens"), split_axis=0, concat_axis=0, tiled=True)
-    tab_all = lax.all_to_all(tab_copies, "lon", split_axis=0, concat_axis=0, tiled=True)
+    twin = lax.ppermute(tab_all, "ens", [(0, 1), (1, 0)])
     half = call(band_sum_kernel, near((PART, 128), BF16), near=1)(bands)
     other = lax.ppermute(half, "core", [(0, 1), (1, 0)])
     qw, pw, f1, f2, qb, pb, f1b, f2b, n1g, n1o, n2g, n2o = call(
@@ -555,9 +561,7 @@
         near=2,
         scratch=[pltpu.VMEM((2, PART, 128), F32)],
     )(core, half, other)
-    tab_out = call(table_kernel, shape((12 * ROWS, 23), F32), near=1)(
-        tab_all.reshape(16 * SLOT, 128)
-    )
+    tab_out = call(table_kernel, shape((12 * ROWS, 23), F32), near=2)(tab_all, twin)
     full = both.reshape(2, *grid[1:])
     ends = home.reshape(2, grid[1], grid[2], 8, C)[:, :, :, :6]
     full = jnp.concatenate([ends, full[:, :, :, 6:]], axis=3)

time: 87.9 us -> 85.7 us (0.975)
  the two profiles are of different devices: /device:TPU:2 before, /device:TPU:1 now
where the time goes in v3:
time: 85.7 us; the launch traced here: 85.5 us
  blocking collectives  34.2 us (40%)
  starting transfers between devices  26.3 us (31%)
  Pallas kernels  20.4 us (24%)
  waiting for transfers between devices  2.21 us (3%)
  other arithmetic  1.1 us (1%)
  between operations  1 us (1%)
    all_to_all x1, blocking collectives, on_device(): lax.all_to_all(joined, 'lon', split_axis=0, concat_axis=0, tiled=True)  21.1 us
    pallas_call x10, Pallas kernels, go(): return run(*kept)  20.4 us
    all_to_all x1, blocking collectives, on_device(): tab = lax.all_to_all(tab, 'lon', split_axis=0, concat_axis=0, tiled=True)  13 us
    ppermute x1, starting transfers between devices, on_device(): halo = lax.ppermute(edge, 'lon', [(k, (k - 1) % 16) for k in range(16)])  7.4 us
    ppermute x1, starting transfers between devices, on_device(): other = lax.ppermute(half, 'core', [(0, 1), (1, 0)])  6.54 us
    all_to_all x1, starting transfers between devices, on_device(): lax.all_to_all(part, ('y', 'ens'), split_axis=0, concat_axis=0, tiled=True)  6.35 us
    ppermute x1, starting transfers between devices, on_device(): twin = lax.ppermute(tab_all, 'ens', [(0, 1), (1, 0)])  2.97 us
    all_to_all x1, waiting for transfers between devices, on_device(): lax.all_to_all(part, ('y', 'ens'), split_axis=0, concat_axis=0, tiled=True)  2.05 us
  transfers between devices with their start and end apart: 6, of which 2 were waited for; matrix products, arithmetic and copies ran while one was open for 2% of the time, Pallas kernels for 6%

profile of v3, /device:TPU:1, one launch (start us, length us, event | category | flops | bytes accessed | tf_op | source)
XLA Modules:
  0.0 85.5 jit_solution(6124121384342269041)
XLA Ops:
  0.6 0.0 copy-start
  0.7 0.0 copy-start.1
  0.7 0.0 copy-start.2
  0.7 0.0 copy-start.3
  0.7 0.0 copy-start.4
  0.7 0.0 copy-start.5
  0.7 0.0 copy-start.6
  0.7 0.0 copy-start.7
  0.7 0.0 copy-start.8
  0.7 0.0 copy-start.9
  0.7 1.0 %shard_map.262 = bf16[2,24,8,192]{3,2,1,0:T(8,128)(2,1)S(1)} custom-call(bf16[24,24,192]{2,1,0:T(8,128)(2,1)} %bitcast.16, bf16[24,24,192]{2,1,0:T(8,128)(2,1)} %bitcast.18), custom_call_target="tpu_custom_call" | custom-call | tf_op jit(solution)/shard_map/pallas_call | solution.py:481
  1.8 7.4 %collective-permute-start = (bf16[2,192,192]{2,1,0:T(8,128)(2,1)S(1)}, bf16[2,192,192]{2,1,0:T(8,128)(2,1)S(1)}, u32[]{:S(2)}, u32[]{:S(2)}) collective-permute-start(bf16[2,192,192]{2,1,0:T(8,128)(2,1)S(1)} %bitcast.21), channel_id=1, source_target_pairs={{0,240},{16,0},{32,16},{48,32},{64,48},{80,64},{96,80},{112,96},{1... | collective-permute-start | bytes 442376 | tf_op jit(solution)/shard_map/ppermute | solution.py:504
  9.2 3.4 %shard_map.263 = (bf16[576,192]{1,0:T(8,128)(2,1)S(1)}, bf16[192,192]{1,0:T(8,128)(2,1)S(1)}, bf16[192,768]{1,0:T(8,128)(2,1)S(1)}, bf16[192,768]{1,0:T(8,128)(2...) custom-call(f32[192,576]{1,0:T(8,128)} %qkv_hbm.1, ...), custom_call_target="tpu_custom_call" | custom-call | tf_op jit(solution)/shard_map/pallas_call | solution.py:481
  12.6 0.2 collective-permute-done.halo_ref
  12.8 0.0 copy-done
  12.8 0.0 copy-done.1
  12.8 0.0 copy-done.2
  12.8 0.0 copy-done.3
  12.8 0.0 copy-done.4
  12.8 0.0 copy-done.5
  12.8 0.0 copy-done.6
  12.8 0.0 copy-done.7
  12.8 0.0 copy-done.8
  12.8 0.0 copy-done.9
  12.8 10.8 %shard_map.264 = (bf16[16,32,128]{2,1,0:T(8,128)(2,1)S(1)}, bf16[576,192]{1,0:T(8,128)(2,1)S(1)}, bf16[8,576,192]{2,1,0:T(8,128)(2,1)S(1)}, bf16[2,576,768]{2,1,...) custom-call(bf16[576,192]{1,0:T(8,128)(2,1)S(1)} %bitcast.17, ...), custom_call_target="tpu_custom_call" | custom-call | tf_op jit(solution)/shard_map/pallas_call | solution.py:481
  23.6 1.6 %shard_map.265 = (bf16[576,192]{1,0:T(8,128)(2,1)S(1)}, bf16[1792,128]{1,0:T(8,128)(2,1)S(1)}, bf16[1792,128]{1,0:T(8,128)(2,1)S(1)}, bf16[16,32,128]{2,1,0:T(8,128)(2,1)S(1)}) custom-call(s32[1]{0:T(128)} %bitcast.7.core_ref, f32[192]{0:T(256)S(1)} %copy-done.4, bf16[8,576,192]{2,1,0:T(8,128)(2,1)S(1)} %get-tuple-element.68.few_ref, ...), custom_call_target="tpu_custom_call" | custom-call | tf_op jit(solution)/shard_map/pallas_call | solution.py:481
  25.2 1.6 %collective-permute-start.2 = (bf16[1792,128]{1,0:T(8,128)(2,1)S(1)}, bf16[1792,128]{1,0:T(8,128)(2,1)S(1)}, u32[]{:S(2)}, u32[]{:S(2)}) collective-permute-start(bf16[1792,128]{1,0:T(8,128)(2,1)S(1)} %get-tuple-element.85), channel_id=1, source_target_pairs={{0,2},{2,0},{1,3},{3,1},{4,6},{6,4},{5,7},{7,5},{8,10},{10,8},{9,1... | collective-permute-start | bytes 1376264 | tf_op jit(solution)/shard_map/ppermute | solution.py:542
  26.9 13.0 %all_to_all.15.tab_ref = bf16[16,32,128]{2,1,0:T(8,128)(2,1)S(1)} all-to-all(bf16[16,32,128]{2,1,0:T(8,128)(2,1)S(1)} %get-tuple-element.86), channel_id=1, replica_groups=mesh['lon'=16,'y'=4,'core'=2,'ens'=2] {'lon'}, dimensions={0} | all-to-all | bytes 262144 | tf_op jit(solution)/shard_map/all_to_all | solution.py:541
  39.9 0.0 collective-permute-done.2.got_ref
  39.9 0.1 shard_map.267
  40.0 21.1 %all_to_all.16.in_ref = bf16[16,144,128]{2,1,0:T(8,128)(2,1)S(1)} all-to-all(bf16[16,144,128]{2,1,0:T(8,128)(2,1)S(1)} %shard_map.267), channel_id=1, replica_groups=mesh['lon'=16,'y'=4,'core'=2,'ens'=2] {'lon'}, dimensions={0} | all-to-all | bytes 1179648 | tf_op jit(solution)/shard_map/all_to_all | solution.py:544
  61.2 0.8 shard_map.268
  61.9 6.4 %all-to-all-start.2 = ((bf16[8,112,128]{2,1,0:T(8,128)(2,1)}), bf16[8,112,128]{2,1,0:T(8,128)(2,1)S(1)}, u32[]{:S(2)}, u32[]{:S(2)}) async-start(bf16[8,112,128]{2,1,0:T(8,128)(2,1)} %get-tuple-element.87), calls=%async_computation.2 | async-start | bytes 458752 | tf_op jit(solution)/shard_map/all_to_all | solution.py:552
  68.3 0.8 shard_map.266
  69.0 1.4 %collective-permute-start.1 = (bf16[2,192,192]{2,1,0:T(8,128)(2,1)S(1)}, bf16[2,192,192]{2,1,0:T(8,128)(2,1)S(1)}, u32[]{:S(2)}, u32[]{:S(2)}) collective-permute-start(bf16[2,192,192]{2,1,0:T(8,128)(2,1)S(1)} %get-tuple-element.82), channel_id=1, source_target_pairs={{0,16},{16,32},{32,48},{48,64},{64,80},{80,96},{96,112},{112,128},... | collective-permute-start | bytes 442376 | tf_op jit(solution)/shard_map/ppermute | solution.py:548
  70.4 3.0 %collective-permute-start.4 = (bf16[512,128]{1,0:T(8,128)(2,1)S(1)}, bf16[512,128]{1,0:T(8,128)(2,1)S(1)}, u32[]{:S(2)}, u32[]{:S(2)}) collective-permute-start(bf16[512,128]{1,0:T(8,128)(2,1)S(1)} %get-tuple-element.100.tab_ref), channel_id=1, source_target_pairs={{0,1},{1,0},{2,3},{3,2},{4,5},{5,4},{6,7},{7,6},{8,9},{9,8},{10,11... | collective-permute-start | bytes 393224 | tf_op jit(solution)/shard_map/ppermute | solution.py:553
  73.4 0.3 slice.17
  73.7 2.1 %all-to-all-done.2.in_ref = bf16[8,112,128]{2,1,0:T(8,128)(2,1)S(1)} async-done(((bf16[8,112,128]{2,1,0:T(8,128)(2,1)}), bf16[8,112,128]{2,1,0:T(8,128)(2,1)S(1)}, u32[]{:S(2)}, u32[]{:S(2)}) %all-to-all-start.2) | async-done | bytes 229408 | tf_op jit(solution)/shard_map/all_to_all | solution.py:552
  75.8 6.5 %collective-permute-start.3 = (bf16[112,128]{1,0:T(8,128)(2,1)S(1)}, bf16[112,128]{1,0:T(8,128)(2,1)S(1)}, u32[]{:S(2)}, u32[]{:S(2)}) collective-permute-start(bf16[112,128]{1,0:T(8,128)(2,1)S(1)} %shard_map.269.own_ref), channel_id=1, source_target_pairs={{0,2},{2,0},{1,3},{3,1},{4,6},{6,4},{5,7},{7,5},{8,10},{10,8},{9,1... | collective-permute-start | bytes 86024 | tf_op jit(solution)/shard_map/ppermute | solution.py:555
  82.3 0.0 collective-permute-done.1
  82.3 1.1 %pad_maximum_fusion = (bf16[1,4,6,24,192]{4,3,2,1,0:T(8,128)(2,1)}, bf16[1,4,6,24,192]{4,3,2,1,0:T(8,128)(2,1)}) fusion(bf16[2,4,6,18,192]{4,3,2,1,0:T(8,128)(2,1)S(1)} %slice.17, bf16[2,4,6,6,192]{4,3,2,1,0:T(8,128)(2,1)S(1)} %bitcast.25), kind=kLoop, calls=%fused_computation.3 | loop fusion | flops 884736 | bytes 884736 | tf_op jit(solution)/shard_map/concatenate | solution.py:567
  83.4 0.0 collective-permute-done.4.twin_ref
  83.4 1.2 %shard_map.271 = f32[1728,23]{1,0:T(8,128)} custom-call(bf16[512,128]{1,0:T(8,128)(2,1)S(1)} %get-tuple-element.100.tab_ref, bf16[512,128]{1,0:T(8,128)(2,1)S(1)} %collective-permute-done.4.twin_ref), custom_call_target="tpu_custom_call" | custom-call | tf_op jit(solution)/shard_map/pallas_call | solution.py:481
  84.6 0.0 collective-permute-done.3.got_ref
  84.6 0.7 shard_map.270
  (1 shorter events, 0.0 us)
Async XLA Ops:
  0.6 12.1 %copy-start = (bf16[1,4,6,24,192]{4,3,2,1,0:T(8,128)(2,1)S(1)}, bf16[1,4,6,24,192]{4,3,2,1,0:T(8,128)(2,1)}, u32[]{:S(2)}) copy-start(bf16[1,4,6,24,192]{4,3,2,1,0:T(8,128)(2,1)} %param.15) | copy-start | bytes 663556
  0.7 12.1 %copy-start.1 = (bf16[1,4,6,24,192]{4,3,2,1,0:T(8,128)(2,1)S(1)}, bf16[1,4,6,24,192]{4,3,2,1,0:T(8,128)(2,1)}, u32[]{:S(2)}) copy-start(bf16[1,4,6,24,192]{4,3,2,1,0:T(8,128)(2,1)} %param.16) | copy-start | bytes 663556
  0.7 12.1 %copy-start.2 = (f32[576]{0:T(1024)S(1)}, f32[576]{0:T(1024)}, u32[]{:S(2)}) copy-start(f32[576]{0:T(1024)} %qb_ref.1) | copy-start | bytes 6916
  0.7 12.1 %copy-start.3 = (f32[768]{0:T(1024)S(1)}, f32[768]{0:T(1024)}, u32[]{:S(2)}) copy-start(f32[768]{0:T(1024)} %f1b_ref.1) | copy-start | bytes 9220
  0.7 12.1 %copy-start.4 = (f32[192]{0:T(256)S(1)}, f32[192]{0:T(256)}, u32[]{:S(2)}) copy-start(f32[192]{0:T(256)} %n1g_ref.3) | copy-start | bytes 2308
  0.7 12.1 %copy-start.5 = (f32[192]{0:T(256)S(1)}, f32[192]{0:T(256)}, u32[]{:S(2)}) copy-start(f32[192]{0:T(256)} %n1o_ref.1) | copy-start | bytes 2308
  0.7 12.1 %copy-start.6 = (f32[192]{0:T(256)S(1)}, f32[192]{0:T(256)}, u32[]{:S(2)}) copy-start(f32[192]{0:T(256)} %pb_ref.1) | copy-start | bytes 2308
  0.7 12.1 %copy-start.7 = (f32[192]{0:T(256)S(1)}, f32[192]{0:T(256)}, u32[]{:S(2)}) copy-start(f32[192]{0:T(256)} %n2g_ref.1) | copy-start | bytes 2308
  0.7 12.1 %copy-start.8 = (f32[192]{0:T(256)S(1)}, f32[192]{0:T(256)}, u32[]{:S(2)}) copy-start(f32[192]{0:T(256)} %n2o_ref.1) | copy-start | bytes 2308
  0.7 12.1 %copy-start.9 = (f32[192]{0:T(256)S(1)}, f32[192]{0:T(256)}, u32[]{:S(2)}) copy-start(f32[192]{0:T(256)} %f2b_ref.1) | copy-start | bytes 2308
  1.8 11.0 %collective-permute-start = (bf16[2,192,192]{2,1,0:T(8,128)(2,1)S(1)}, bf16[2,192,192]{2,1,0:T(8,128)(2,1)S(1)}, u32[]{:S(2)}, u32[]{:S(2)}) collective-permute-start(bf16[2,192,192]{2,1,0:T(8,128)(2,1)S(1)} %bitcast.21), channel_id=1, source_target_pairs={{0,240},{16,0},{32,16},{48,32},{64,48},{80,64},{96,80},{112,96},{1... | collective-permute-start | bytes 442376 | tf_op jit(solution)/shard_map/ppermute | solution.py:504
  25.2 14.6 %collective-permute-start.2 = (bf16[1792,128]{1,0:T(8,128)(2,1)S(1)}, bf16[1792,128]{1,0:T(8,128)(2,1)S(1)}, u32[]{:S(2)}, u32[]{:S(2)}) collective-permute-start(bf16[1792,128]{1,0:T(8,128)(2,1)S(1)} %get-tuple-element.85), channel_id=1, source_target_pairs={{0,2},{2,0},{1,3},{3,1},{4,6},{6,4},{5,7},{7,5},{8,10},{10,8},{9,1... | collective-permute-start | bytes 1376264 | tf_op jit(solution)/shard_map/ppermute | solution.py:542
  61.9 13.8 %all-to-all-start.2 = ((bf16[8,112,128]{2,1,0:T(8,128)(2,1)}), bf16[8,112,128]{2,1,0:T(8,128)(2,1)S(1)}, u32[]{:S(2)}, u32[]{:S(2)}) async-start(bf16[8,112,128]{2,1,0:T(8,128)(2,1)} %get-tuple-element.87), calls=%async_computation.2 | async-start | bytes 458752 | tf_op jit(solution)/shard_map/all_to_all | solution.py:552
  69.0 13.3 %collective-permute-start.1 = (bf16[2,192,192]{2,1,0:T(8,128)(2,1)S(1)}, bf16[2,192,192]{2,1,0:T(8,128)(2,1)S(1)}, u32[]{:S(2)}, u32[]{:S(2)}) collective-permute-start(bf16[2,192,192]{2,1,0:T(8,128)(2,1)S(1)} %get-tuple-element.82), channel_id=1, source_target_pairs={{0,16},{16,32},{32,48},{48,64},{64,80},{80,96},{96,112},{112,128},... | collective-permute-start | bytes 442376 | tf_op jit(solution)/shard_map/ppermute | solution.py:548
  70.4 13.0 %collective-permute-start.4 = (bf16[512,128]{1,0:T(8,128)(2,1)S(1)}, bf16[512,128]{1,0:T(8,128)(2,1)S(1)}, u32[]{:S(2)}, u32[]{:S(2)}) collective-permute-start(bf16[512,128]{1,0:T(8,128)(2,1)S(1)} %get-tuple-element.100.tab_ref), channel_id=1, source_target_pairs={{0,1},{1,0},{2,3},{3,2},{4,5},{5,4},{6,7},{7,6},{8,9},{9,8},{10,11... | collective-permute-start | bytes 393224 | tf_op jit(solution)/shard_map/ppermute | solution.py:553
  75.8 8.8 %collective-permute-start.3 = (bf16[112,128]{1,0:T(8,128)(2,1)S(1)}, bf16[112,128]{1,0:T(8,128)(2,1)S(1)}, u32[]{:S(2)}, u32[]{:S(2)}) collective-permute-start(bf16[112,128]{1,0:T(8,128)(2,1)S(1)} %shard_map.269.own_ref), channel_id=1, source_target_pairs={{0,2},{2,0},{1,3},{3,1},{4,6},{6,4},{5,7},{7,5},{8,10},{10,8},{9,1... | collective-permute-start | bytes 86024 | tf_op jit(solution)/shard_map/ppermute | solution.py:555

commit v4 on v2

--- a/solution.py
+++ b/solution.py
@@ -217,13 +217,20 @@
     mask = mask_ref[...]
     saved = []
     attended = []
-    for g in range(4):
-        rows = slice(ROWS * g, ROWS * g + ROWS)
-        own = normed[rows]
+
+    def begin(g):
+        own = normed[ROWS * g : ROWS * g + ROWS]
         query_t = (nt(wq, own) + bq).astype(BF16)
         value_t = (nt(wv, own) + bv).astype(BF16)
         query_bd = nn(query_t, spread).astype(BF16) * mask
-        scores = nn(keys[rows], query_bd) * SCALE + bias_ref[g % 2]
+        return query_bd, value_t, nn(keys[ROWS * g : ROWS * g + ROWS], query_bd)
+
+    ahead = begin(0)
+    for g in range(4):
+        query_bd, value_t, raw = ahead
+        if g < 3:
+            ahead = begin(g + 1)
+        scores = raw * SCALE + bias_ref[g % 2]
         peak = jnp.max(scores, axis=0, keepdims=True)
         raised = jnp.exp(scores - peak)
         total = jnp.sum(raised, axis=0, keepdims=True)
@@ -239,15 +246,22 @@
     acts = []
     grads = []
     f1_sums = []
+
+    def feed(g):
+        rows = slice(ROWS * g, ROWS * g + ROWS)
+        return nn(normed2[rows], fc1_ref[...]), nn(cot_low[rows], fc2_ref[...])
+
+    ahead = feed(0)
     for g in range(4):
-        rows = slice(ROWS * g, ROWS * g + ROWS)
-        u = nn(normed2[rows], fc1_ref[...]) + f1b
+        u, act_grad = ahead
+        if g < 3:
+            ahead = feed(g + 1)
+        u = u + f1b
         square = u * u
         half = 0.5 * jnp.tanh(u * (GELU_C + (GELU_A * GELU_C) * square)) + 0.5
         acts.append((u * half).astype(BF16))
         lean = u * (2.0 * GELU_C + (6.0 * GELU_A * GELU_C) * square)
         slope = half + (half - half * half) * lean
-        act_grad = nn(cot_low[rows], fc2_ref[...])
         pre = (act_grad * slope).astype(BF16)
         grads.append(pre)
         f1_sums.append(jnp.sum(pre.astype(F32), axis=0, keepdims=True))
@@ -266,13 +280,20 @@
     grad_q = []
     grad_k = []
     grad_v = []
-    for g in range(4):
+
+    def reach(g):
         rows = slice(ROWS * g, ROWS * g + ROWS)
-        query_bd, weights = saved[g]
-        own = normed[rows]
         grad_t = nt(proj_ref[...], attn_grad[rows]).astype(BF16)
         grad_bd = nn(grad_t, spread).astype(BF16) * mask
-        prob_grad = nn(values[rows], grad_bd)
+        return grad_bd, nn(values[rows], grad_bd)
+
+    ahead = reach(0)
+    for g in range(4):
+        query_bd, weights = saved[g]
+        own = normed[ROWS * g : ROWS * g + ROWS]
+        grad_bd, prob_grad = ahead
+        if g < 3:
+            ahead = reach(g + 1)
         probs = weights.astype(F32)
         shared = jnp.sum(probs * prob_grad, axis=0, keepdims=True)
         score_grad = probs * (prob_grad - shared)
@@ -392,30 +413,31 @@
         copy.wait()
 
 
-def join_kernel(own_ref, got_ref, tab_ref, twin_ref, out_ref):
+def join_kernel(own_ref, got_ref, tab_ref, out_ref):
     for l in range(16):
         part = slice(PART * l, PART * l + PART)
         out_ref[l, 0:PART, :] = (own_ref[part].astype(F32) + got_ref[part].astype(F32)).astype(BF16)
-        spot = slice(SLOT * l, SLOT * l + SLOT)
-        out_ref[l, PART:, :] = (tab_ref[spot].astype(F32) + twin_ref[spot].astype(F32)).astype(BF16)
-
-
-def lon_sum_kernel(in_ref, part_ref, tab_ref):
+        out_ref[l, PART:, :] = tab_ref[SLOT * l : SLOT * l + SLOT]
+
+
+def lon_sum_kernel(in_ref, out_ref):
     total = in_ref[0].astype(F32)
     for l in range(1, 16):
         total = total + in_ref[l].astype(F32)
     low = total.astype(BF16)
     for k in range(8):
-        part_ref[k] = low[:PART]
-    for k in range(16):
-        tab_ref[k] = low[PART:]
-
-
-def band_sum_kernel(in_ref, out_ref):
-    total = in_ref[0].astype(F32)
+        out_ref[k] = low
+
+
+def band_sum_kernel(y_ref, in_ref, out_ref, tab_ref):
+    total = in_ref[0, 0:PART].astype(F32)
     for k in range(1, 8):
-        total = total + in_ref[k].astype(F32)
+        total = total + in_ref[k, 0:PART].astype(F32)
     out_ref[...] = total.astype(BF16)
+    y = y_ref[0]
+    low = (in_ref[2 * y, PART:].astype(F32) + in_ref[2 * y + 1, PART:].astype(F32)).astype(BF16)
+    for l in range(16):
+        tab_ref[l] = low
 
 
 def weight_kernel(core_ref, own_ref, got_ref, qw_ref, pw_ref, f1_ref, f2_ref, qb_ref, pb_ref, f1b_ref,
@@ -523,7 +545,6 @@
         scratch=[pltpu.VMEM((2, ROWS, LANES), F32), pltpu.VMEM((16 * SLOT, 128), F32)],
     )(x, cot, norm1_gain, norm1_offset, qkv_bias, proj_bias, norm2_gain, norm2_offset, fc1_bias,
       fc2_bias, halo, bias, wt, proj, fc1, fc2, spread, mask, sel, picks)
-    twin = lax.ppermute(tab, "ens", [(0, 1), (1, 0)])
     slope, own, send = call(
         back_kernel,
         [near((576, C), BF16), near((16 * PART, 128), BF16), near((16 * PART, 128), BF16)],
@@ -534,18 +555,19 @@
         scratch=[pltpu.VMEM((2, 16 * PART, 128), F32)],
     )(core, norm1_gain, *state, wt, ra, ca, rb, cb)
     got = lax.ppermute(send, "core", [(0, 1), (1, 0)])
-    joined = call(join_kernel, near((16, PART + SLOT, 128), BF16), near=4)(own, got, tab, twin)
+    joined = call(join_kernel, near((16, PART + SLOT, 128), BF16), near=3)(own, got, tab)
     arrived = lax.all_to_all(joined, "lon", split_axis=0, concat_axis=0, tiled=True)
     both, ends = call(
         place_kernel, [near((2, 576, C), BF16), near((2, 192, C), BF16)], near=3
     )(block, slope, back)
     home = lax.ppermute(ends, "lon", [(k, (k + 1) % 16) for k in range(16)])
-    part, tab_copies = call(
-        lon_sum_kernel, [near((8, PART, 128), BF16), near((16, SLOT, 128), BF16)], near=1
-    )(arrived)
-    bands = lax.all_to_all(part, ("y", "ens"), split_axis=0, concat_axis=0, tiled=True)
+    copies = call(lon_sum_kernel, near((8, PART + SLOT, 128), BF16), near=1)(arrived)
+    bands = lax.all_to_all(copies, ("y", "ens"), split_axis=0, concat_axis=0, tiled=True)
+    band = lax.axis_index("y").astype(jnp.int32).reshape(1)
+    half, tab_copies = call(
+        band_sum_kernel, [near((PART, 128), BF16), near((16, SLOT, 128), BF16)], smem=1, near=1
+    )(band, bands)
     tab_all = lax.all_to_all(tab_copies, "lon", split_axis=0, concat_axis=0, tiled=True)
-    half = call(band_sum_kernel, near((PART, 128), BF16), near=1)(bands)
     other = lax.ppermute(half, "core", [(0, 1), (1, 0)])
     qw, pw, f1, f2, qb, pb, f1b, f2b, n1g, n1o, n2g, n2o = call(
         weight_kernel,

time: 87.9 us -> 83.9 us (0.954)
  starting transfers between devices: 20.4 us -> 17.9 us
  waiting for transfers between devices: 19.6 us -> 17.3 us
    ppermute x1 -> x0, waiting for transfers between devices: 4.88 us -> none  [on_device(): twin = lax.ppermute(tab, 'ens', [(0, 1), (1, 0)])]
    ppermute x1 -> x0, starting transfers between devices: 2.52 us -> none  [on_device(): twin = lax.ppermute(tab, 'ens', [(0, 1), (1, 0)])]
    ppermute x1, waiting for transfers between devices: 0.01 us -> 1.8 us  [on_device(): got = lax.ppermute(send, 'core', [(0, 1), (1, 0)])]
  transfers between devices with their start and end apart: 7 -> 6, of which waited for: 5 -> 5; matrix products, arithmetic and copies ran while one was open for 2% -> 2% of each run, Pallas kernels for 6% -> 7%
where the time goes in v4:
time: 83.9 us; the launch traced here: 83.6 us
  blocking collectives  25.5 us (30%)
  Pallas kernels  20.6 us (25%)
  starting transfers between devices  17.9 us (21%)
  waiting for transfers between devices  17.3 us (21%)
  other arithmetic  1.11 us (1%)
  between operations  0.86 us (1%)
    all_to_all x1, blocking collectives, on_device(): lax.all_to_all(joined, 'lon', split_axis=0, concat_axis=0, tiled=True)  25.5 us
    pallas_call x10, Pallas kernels, go(): return run(*kept)  20.6 us
    all_to_all x1, waiting for transfers between devices, on_device(): lax.all_to_all(copies, ('y', 'ens'), split_axis=0, concat_axis=0, tiled=T...  9.42 us
    all_to_all x1, starting transfers between devices, on_device(): lax.all_to_all(copies, ('y', 'ens'), split_axis=0, concat_axis=0, tiled=T...  6.03 us
    ppermute x1, starting transfers between devices, on_device(): halo = lax.ppermute(edge, 'lon', [(k, (k - 1) % 16) for k in range(16)])  5.9 us
    all_to_all x1, waiting for transfers between devices, on_device(): lax.all_to_all(tab_copies, 'lon', split_axis=0, concat_axis=0, tiled=True)  5.3 us
    all_to_all x1, starting transfers between devices, on_device(): lax.all_to_all(tab_copies, 'lon', split_axis=0, concat_axis=0, tiled=True)  4.92 us
    ppermute x1, waiting for transfers between devices, on_device(): got = lax.ppermute(send, 'core', [(0, 1), (1, 0)])  1.8 us
  transfers between devices with their start and end apart: 6, of which 5 were waited for; matrix products, arithmetic and copies ran while one was open for 2% of the time, Pallas kernels for 7%

profile of v4, /device:TPU:2, one launch (start us, length us, event | category | flops | bytes accessed | tf_op | source)
XLA Modules:
  0.0 83.6 jit_solution(3583960792238335374)
XLA Ops:
  0.6 0.0 copy-start
  0.7 0.0 copy-start.1
  0.7 0.0 copy-start.2
  0.7 0.0 copy-start.3
  0.7 0.0 copy-start.4
  0.7 0.0 copy-start.5
  0.7 0.0 copy-start.6
  0.7 0.0 copy-start.7
  0.7 0.0 copy-start.8
  0.7 0.0 copy-start.9
  0.7 1.0 %shard_map.262 = bf16[2,24,8,192]{3,2,1,0:T(8,128)(2,1)S(1)} custom-call(bf16[24,24,192]{2,1,0:T(8,128)(2,1)} %bitcast.18, bf16[24,24,192]{2,1,0:T(8,128)(2,1)} %bitcast.20), custom_call_target="tpu_custom_call" | custom-call | tf_op jit(solution)/shard_map/pallas_call | solution.py:498
  1.8 5.9 %collective-permute-start = (bf16[2,192,192]{2,1,0:T(8,128)(2,1)S(1)}, bf16[2,192,192]{2,1,0:T(8,128)(2,1)S(1)}, u32[]{:S(2)}, u32[]{:S(2)}) collective-permute-start(bf16[2,192,192]{2,1,0:T(8,128)(2,1)S(1)} %bitcast.24), channel_id=1, source_target_pairs={{0,240},{16,0},{32,16},{48,32},{64,48},{80,64},{96,80},{112,96},{1... | collective-permute-start | bytes 442376 | tf_op jit(solution)/shard_map/ppermute | solution.py:521
  7.7 3.4 %shard_map.263 = (bf16[576,192]{1,0:T(8,128)(2,1)S(1)}, bf16[192,192]{1,0:T(8,128)(2,1)S(1)}, bf16[192,768]{1,0:T(8,128)(2,1)S(1)}, bf16[192,768]{1,0:T(8,128)(2...) custom-call(f32[192,576]{1,0:T(8,128)} %qkv_hbm.1, ...), custom_call_target="tpu_custom_call" | custom-call | tf_op jit(solution)/shard_map/pallas_call | solution.py:498
  11.1 0.7 collective-permute-done.halo_ref
  11.8 0.0 copy-done
  11.8 0.0 copy-done.1
  11.8 0.0 copy-done.2
  11.8 0.0 copy-done.3
  11.8 0.0 copy-done.4
  11.9 0.0 copy-done.5
  11.9 0.0 copy-done.6
  11.9 0.0 copy-done.7
  11.9 0.0 copy-done.8
  11.9 0.0 copy-done.9
  11.9 10.4 %shard_map.264 = (bf16[512,128]{1,0:T(8,128)(2,1)S(1)}, bf16[576,192]{1,0:T(8,128)(2,1)S(1)}, bf16[8,576,192]{2,1,0:T(8,128)(2,1)S(1)}, bf16[2,576,768]{2,1,0:T(...) custom-call(bf16[576,192]{1,0:T(8,128)(2,1)S(1)} %bitcast.19, ...), custom_call_target="tpu_custom_call" | custom-call | tf_op jit(solution)/shard_map/pallas_call | solution.py:498
  22.3 1.6 %shard_map.265 = (bf16[576,192]{1,0:T(8,128)(2,1)S(1)}, bf16[1792,128]{1,0:T(8,128)(2,1)S(1)}, bf16[1792,128]{1,0:T(8,128)(2,1)S(1)}) custom-call(s32[1]{0:T(128)} %bitcast.7.core_ref, f32[192]{0:T(256)S(1)} %copy-done.4, bf16[8,576,192]{2,1,0:T(8,128)(2,1)S(1)} %get-tuple-element.67.few_ref, bf16[2,576,768]{2,1,0:T(8,128)(2,1)S(1)} %get-tuple-element.68.wide_ref, ...), custom_call_target="tpu_custom_call" | custom-call | tf_op jit(solution)/shard_map/pallas_call | solution.py:498
  23.9 0.1 collective-permute-start.2
  24.0 1.8 %collective-permute-done.2.got_ref = bf16[1792,128]{1,0:T(8,128)(2,1)S(1)} collective-permute-done((bf16[1792,128]{1,0:T(8,128)(2,1)S(1)}, bf16[1792,128]{1,0:T(8,128)(2,1)S(1)}, u32[]{:S(2)}, u32[]{:S(2)}) %collective-permute-start.2) | collective-permute-done | bytes 458784 | tf_op jit(solution)/shard_map/ppermute | solution.py:557
  25.8 0.1 shard_map.267
  25.9 25.5 %all_to_all.15.in_ref = bf16[16,144,128]{2,1,0:T(8,128)(2,1)S(1)} all-to-all(bf16[16,144,128]{2,1,0:T(8,128)(2,1)S(1)} %shard_map.267), channel_id=1, replica_groups=mesh['lon'=16,'y'=4,'core'=2,'ens'=2] {'lon'}, dimensions={0} | all-to-all | bytes 1179648 | tf_op jit(solution)/shard_map/all_to_all | solution.py:559
  51.4 0.8 shard_map.268
  52.2 6.0 %all-to-all-start.1 = ((bf16[8,144,128]{2,1,0:T(8,128)(2,1)}), bf16[8,144,128]{2,1,0:T(8,128)(2,1)S(1)}, u32[]{:S(2)}, u32[]{:S(2)}) async-start(bf16[8,144,128]{2,1,0:T(8,128)(2,1)} %shard_map.268), calls=%async_computation.1 | async-start | bytes 589824 | tf_op jit(solution)/shard_map/all_to_all | solution.py:565
  58.3 0.8 shard_map.266
  59.0 0.9 %collective-permute-start.1 = (bf16[2,192,192]{2,1,0:T(8,128)(2,1)S(1)}, bf16[2,192,192]{2,1,0:T(8,128)(2,1)S(1)}, u32[]{:S(2)}, u32[]{:S(2)}) collective-permute-start(bf16[2,192,192]{2,1,0:T(8,128)(2,1)S(1)} %get-tuple-element.80), channel_id=1, source_target_pairs={{0,16},{16,32},{32,48},{48,64},{64,80},{80,96},{96,112},{112,128},... | collective-permute-start | bytes 442376 | tf_op jit(solution)/shard_map/ppermute | solution.py:563
  59.9 9.4 %all-to-all-done.1.in_ref = bf16[8,144,128]{2,1,0:T(8,128)(2,1)S(1)} async-done(((bf16[8,144,128]{2,1,0:T(8,128)(2,1)}), bf16[8,144,128]{2,1,0:T(8,128)(2,1)S(1)}, u32[]{:S(2)}, u32[]{:S(2)}) %all-to-all-start.1) | async-done | bytes 294944 | tf_op jit(solution)/shard_map/all_to_all | solution.py:565
  69.3 0.7 shard_map.269
  70.0 4.9 %all-to-all-start.2 = ((bf16[16,32,128]{2,1,0:T(8,128)(2,1)}), bf16[16,32,128]{2,1,0:T(8,128)(2,1)S(1)}, u32[]{:S(2)}, u32[]{:S(2)}) async-start(bf16[16,32,128]{2,1,0:T(8,128)(2,1)} %get-tuple-element.98), calls=%async_computation.2 | async-start | bytes 262144 | tf_op jit(solution)/shard_map/all_to_all | solution.py:570
  74.9 0.3 slice.17
  75.2 0.1 collective-permute-start.3
  75.3 0.0 collective-permute-done.1
  75.3 1.1 %pad_maximum_fusion = (bf16[1,4,6,24,192]{4,3,2,1,0:T(8,128)(2,1)}, bf16[1,4,6,24,192]{4,3,2,1,0:T(8,128)(2,1)}) fusion(bf16[2,4,6,18,192]{4,3,2,1,0:T(8,128)(2,1)S(1)} %slice.17, bf16[2,4,6,6,192]{4,3,2,1,0:T(8,128)(2,1)S(1)} %bitcast.28), kind=kLoop, calls=%fused_computation.3 | loop fusion | flops 884736 | bytes 884736 | tf_op jit(solution)/shard_map/concatenate | solution.py:585
  76.4 0.1 collective-permute-done.3.got_ref
  76.5 0.7 shard_map.270
  77.2 5.3 %all-to-all-done.2 = bf16[16,32,128]{2,1,0:T(8,128)(2,1)S(1)} async-done(((bf16[16,32,128]{2,1,0:T(8,128)(2,1)}), bf16[16,32,128]{2,1,0:T(8,128)(2,1)S(1)}, u32[]{:S(2)}, u32[]{:S(2)}) %all-to-all-start.2) | async-done | bytes 131104 | tf_op jit(solution)/shard_map/all_to_all | solution.py:570
  82.5 1.1 %shard_map.271 = f32[1728,23]{1,0:T(8,128)} custom-call(bf16[512,128]{1,0:T(8,128)(2,1)S(1)} %bitcast.23), custom_call_target="tpu_custom_call" | custom-call | tf_op jit(solution)/shard_map/pallas_call | solution.py:498
Async XLA Ops:
  0.6 11.2 %copy-start = (bf16[1,4,6,24,192]{4,3,2,1,0:T(8,128)(2,1)S(1)}, bf16[1,4,6,24,192]{4,3,2,1,0:T(8,128)(2,1)}, u32[]{:S(2)}) copy-start(bf16[1,4,6,24,192]{4,3,2,1,0:T(8,128)(2,1)} %param.15) | copy-start | bytes 663556
  0.7 11.2 %copy-start.1 = (bf16[1,4,6,24,192]{4,3,2,1,0:T(8,128)(2,1)S(1)}, bf16[1,4,6,24,192]{4,3,2,1,0:T(8,128)(2,1)}, u32[]{:S(2)}) copy-start(bf16[1,4,6,24,192]{4,3,2,1,0:T(8,128)(2,1)} %param.16) | copy-start | bytes 663556
  0.7 11.2 %copy-start.2 = (f32[576]{0:T(1024)S(1)}, f32[576]{0:T(1024)}, u32[]{:S(2)}) copy-start(f32[576]{0:T(1024)} %qb_ref.1) | copy-start | bytes 6916
  0.7 11.2 %copy-start.3 = (f32[768]{0:T(1024)S(1)}, f32[768]{0:T(1024)}, u32[]{:S(2)}) copy-start(f32[768]{0:T(1024)} %f1b_ref.1) | copy-start | bytes 9220
  0.7 11.2 %copy-start.4 = (f32[192]{0:T(256)S(1)}, f32[192]{0:T(256)}, u32[]{:S(2)}) copy-start(f32[192]{0:T(256)} %n1g_ref.3) | copy-start | bytes 2308
  0.7 11.2 %copy-start.5 = (f32[192]{0:T(256)S(1)}, f32[192]{0:T(256)}, u32[]{:S(2)}) copy-start(f32[192]{0:T(256)} %n1o_ref.1) | copy-start | bytes 2308
  0.7 11.2 %copy-start.6 = (f32[192]{0:T(256)S(1)}, f32[192]{0:T(256)}, u32[]{:S(2)}) copy-start(f32[192]{0:T(256)} %pb_ref.1) | copy-start | bytes 2308
  0.7 11.2 %copy-start.7 = (f32[192]{0:T(256)S(1)}, f32[192]{0:T(256)}, u32[]{:S(2)}) copy-start(f32[192]{0:T(256)} %n2g_ref.1) | copy-start | bytes 2308
  0.7 11.2 %copy-start.8 = (f32[192]{0:T(256)S(1)}, f32[192]{0:T(256)}, u32[]{:S(2)}) copy-start(f32[192]{0:T(256)} %n2o_ref.1) | copy-start | bytes 2308
  0.7 11.2 %copy-start.9 = (f32[192]{0:T(256)S(1)}, f32[192]{0:T(256)}, u32[]{:S(2)}) copy-start(f32[192]{0:T(256)} %f2b_ref.1) | copy-start | bytes 2308
  1.8 10.1 %collective-permute-start = (bf16[2,192,192]{2,1,0:T(8,128)(2,1)S(1)}, bf16[2,192,192]{2,1,0:T(8,128)(2,1)S(1)}, u32[]{:S(2)}, u32[]{:S(2)}) collective-permute-start(bf16[2,192,192]{2,1,0:T(8,128)(2,1)S(1)} %bitcast.24), channel_id=1, source_target_pairs={{0,240},{16,0},{32,16},{48,32},{64,48},{80,64},{96,80},{112,96},{1... | collective-permute-start | bytes 442376 | tf_op jit(solution)/shard_map/ppermute | solution.py:521
  23.9 1.9 %collective-permute-start.2 = (bf16[1792,128]{1,0:T(8,128)(2,1)S(1)}, bf16[1792,128]{1,0:T(8,128)(2,1)S(1)}, u32[]{:S(2)}, u32[]{:S(2)}) collective-permute-start(bf16[1792,128]{1,0:T(8,128)(2,1)S(1)} %get-tuple-element.83), channel_id=1, source_target_pairs={{0,2},{2,0},{1,3},{3,1},{4,6},{6,4},{5,7},{7,5},{8,10},{10,8},{9,1... | collective-permute-start | bytes 1376264 | tf_op jit(solution)/shard_map/ppermute | solution.py:557
  52.2 17.1 %all-to-all-start.1 = ((bf16[8,144,128]{2,1,0:T(8,128)(2,1)}), bf16[8,144,128]{2,1,0:T(8,128)(2,1)S(1)}, u32[]{:S(2)}, u32[]{:S(2)}) async-start(bf16[8,144,128]{2,1,0:T(8,128)(2,1)} %shard_map.268), calls=%async_computation.1 | async-start | bytes 589824 | tf_op jit(solution)/shard_map/all_to_all | solution.py:565
  59.0 16.3 %collective-permute-start.1 = (bf16[2,192,192]{2,1,0:T(8,128)(2,1)S(1)}, bf16[2,192,192]{2,1,0:T(8,128)(2,1)S(1)}, u32[]{:S(2)}, u32[]{:S(2)}) collective-permute-start(bf16[2,192,192]{2,1,0:T(8,128)(2,1)S(1)} %get-tuple-element.80), channel_id=1, source_target_pairs={{0,16},{16,32},{32,48},{48,64},{64,80},{80,96},{96,112},{112,128},... | collective-permute-start | bytes 442376 | tf_op jit(solution)/shard_map/ppermute | solution.py:563
  70.0 12.5 %all-to-all-start.2 = ((bf16[16,32,128]{2,1,0:T(8,128)(2,1)}), bf16[16,32,128]{2,1,0:T(8,128)(2,1)S(1)}, u32[]{:S(2)}, u32[]{:S(2)}) async-start(bf16[16,32,128]{2,1,0:T(8,128)(2,1)} %get-tuple-element.98), calls=%async_computation.2 | async-start | bytes 262144 | tf_op jit(solution)/shard_map/all_to_all | solution.py:570
  75.2 1.3 %collective-permute-start.3 = (bf16[112,128]{1,0:T(8,128)(2,1)S(1)}, bf16[112,128]{1,0:T(8,128)(2,1)S(1)}, u32[]{:S(2)}, u32[]{:S(2)}) collective-permute-start(bf16[112,128]{1,0:T(8,128)(2,1)S(1)} %get-tuple-element.85.own_ref), channel_id=1, source_target_pairs={{0,2},{2,0},{1,3},{3,1},{4,6},{6,4},{5,7},{7,5},{8,10},{10,8},{9,1... | collective-permute-start | bytes 86024 | tf_op jit(solution)/shard_map/ppermute | solution.py:571
